TPU v7x, 32 devices: a whole 2x2x4 slice. The times are simulated.
32 devices in a mesh: seq: 16 (over z, x, core), row: 2 (over y).
Axes of the slice: x: 2, y: 2, z: 4, core: 2. Of those that a mesh axis runs over, the one named last changes fastest.
Arguments:
- patch_queries: bfloat16 [2048, 2048], P('seq', 'row'), may hold values from -15 to 15
- patch_keys: bfloat16 [2048, 2048], P('seq', 'row'), may hold values from -15 to 15
- patch_values: bfloat16 [2048, 2048], P('seq', 'row'), may hold values from -6 to 6
- patch_tasks: int32 [2048], P('seq'), may hold values from 0 to 7
- residual: bfloat16 [2048, 2048], P('seq', 'row'), may hold values from -6 to 6
- output_weight: bfloat16 [2048, 2048], P('row'), may hold values from -0.5 to 0.5
- global_down: bfloat16 [2048, 16], P('row'), may hold values from -0.5 to 0.5
- global_up: bfloat16 [16, 2048], P(None, 'row'), may hold values from -1.5 to 1.5
- global_scales: float32 [8, 16], replicated, may hold values from 0.25 to 4
- local_weight: bfloat16 [2048, 512], P('row'), may hold values from -0.125 to 0.125
- byte_ids: int32 [16384], P('seq'), may hold values from 0 to 255
- byte_table: bfloat16 [256, 512], replicated, may hold values from -6 to 6
- position_table: bfloat16 [8, 512], replicated, may hold values from -6 to 6
- norm_gain: float32 [512], replicated, may hold values from 0.5 to 1.5
- hidden_in: bfloat16 [2048, 512], P('row', 'seq'), may hold values from -0.25 to 0.25
- hidden_out: bfloat16 [2048, 512], P('row', 'seq'), may hold values from -0.125 to 0.125
- local_down: bfloat16 [512, 16], replicated, may hold values from -0.25 to 0.25
- local_up: bfloat16 [16, 2048], P(None, 'row'), may hold values from -1.5 to 1.5
- local_scales: float32 [8, 16], replicated, may hold values from 0.25 to 4
- cotangent: bfloat16 [16384, 512], P(('seq', 'row')), may hold values from -6 to 6
Outputs:
- grad_global_down: float32 [2048, 16], P('row')
- grad_global_up: float32 [16, 2048], P(None, 'row')
- grad_global_scales: float32 [8, 16], replicated
- grad_local_down: float32 [512, 16], replicated
- grad_local_up: float32 [16, 2048], P(None, 'row')
- grad_local_scales: float32 [8, 16], replicated
All inputs are finite; a program needn't handle non-finite values.
Results may differ from a plain program's by a relative error of at most 0.028.
Values may be sent and summed in bfloat16 or wider, within the bound.
A program may use at most 64 MiB of HBM per device.

v0:
```python
import functools
import math

import jax
import jax.numpy as jnp
from jax import lax
from jax.experimental import pallas as pl
from jax.experimental.pallas import tpu as pltpu
from jax.sharding import PartitionSpec as P

HEAD = 128
VOCAB = 256
PATCH = 8
TASKS = 8


def contract(left, right, left_dim, right_dim):
    return lax.dot_general(
        left, right, (((left_dim,), (right_dim,)), ((), ())), preferred_element_type=jnp.float32
    )


def select_rows(table, tasks):
    picks = (tasks[:, None] == jnp.arange(table.shape[0], dtype=jnp.int32)[None, :]).astype(
        jnp.float32
    )
    return jnp.dot(picks, table, precision=lax.Precision.HIGHEST)


def task_totals(tasks, values):
    picks = (tasks[:, None] == jnp.arange(TASKS, dtype=jnp.int32)[None, :]).astype(jnp.float32)
    return lax.dot_general(picks, values, (((0,), (0,)), ((), ())), precision=lax.Precision.HIGHEST)


def gelu_slope(upper):
    cumulative = 0.5 * (1.0 + lax.erf(upper * 0.7071067811865476))
    density = jnp.exp(-0.5 * upper * upper) * 0.3989422804014327
    return cumulative + upper * density


def local_inputs(
    identities, projected, tasks, byte_table, position_table, norm_gain, local_down, local_scales
):
    count = identities.shape[0]
    picks = (identities[:, None] == jnp.arange(VOCAB, dtype=jnp.int32)[None, :]).astype(
        jnp.bfloat16
    )
    embedded = jnp.dot(picks, byte_table, preferred_element_type=jnp.float32)
    patches = count // PATCH
    inputs = (
        embedded.reshape(patches, PATCH, -1)
        + position_table.astype(jnp.float32)[None]
        + projected.astype(jnp.float32)[:, None, :]
    )
    inputs = inputs.reshape(count, -1)
    inverse = lax.rsqrt(jnp.mean(inputs * inputs, axis=1, keepdims=True) + 1e-06)
    normed = (inputs * inverse * norm_gain).astype(jnp.bfloat16)
    lowered = jnp.dot(normed, local_down, preferred_element_type=jnp.float32)
    byte_tasks = jnp.repeat(tasks, PATCH)
    scales = select_rows(local_scales, byte_tasks)
    shrunk = (lowered * scales).astype(jnp.bfloat16)
    return (inputs, inverse, normed, lowered, scales, shrunk, byte_tasks)


def keep_state(current):
    return current


def update_state(state, query_rows, first, key_heads, value_heads, key_places, scale):
    running_max, running_sum, running_out = state
    count = query_rows.shape[0]
    heads = key_heads.shape[1]
    query_heads = query_rows.reshape(count, heads, HEAD)
    scores = (
        jnp.einsum("qhd,khd->hqk", query_heads, key_heads, preferred_element_type=jnp.float32)
        * scale
    )
    query_places = first + jnp.arange(count, dtype=jnp.int32)
    allowed = key_places[None, :] <= query_places[:, None]
    scores = jnp.where(allowed[None], scores, -1e30)
    new_max = jnp.maximum(running_max, jnp.max(scores, axis=2))
    weights = jnp.where(allowed[None], jnp.exp(scores - new_max[:, :, None]), 0.0)
    shrink = jnp.exp(running_max - new_max)
    running_sum = running_sum * shrink + jnp.sum(weights, axis=2)
    mixed = jnp.einsum(
        "hqk,khd->qhd",
        weights.astype(jnp.bfloat16),
        value_heads,
        preferred_element_type=jnp.float32,
    )
    running_out = running_out * jnp.transpose(shrink)[:, :, None] + mixed
    return (new_max, running_sum, running_out)


def finish_state(state):
    running_max, running_sum, running_out = state
    result = running_out / jnp.transpose(running_sum)[:, :, None]
    return result.reshape(result.shape[0], -1).astype(jnp.bfloat16)


def general_body(
    patch_queries,
    patch_keys,
    patch_values,
    patch_tasks,
    residual,
    output_weight,
    global_down,
    global_up,
    global_scales,
    local_weight,
    byte_ids,
    byte_table,
    position_table,
    norm_gain,
    hidden_in,
    hidden_out,
    local_down,
    local_up,
    local_scales,
    cotangent,
):
    rows = patch_queries.shape[0]
    width = patch_queries.shape[1]
    heads = width // HEAD
    row_count = lax.axis_size("row")
    seq_index = lax.axis_index("seq")
    row_index = lax.axis_index("row")
    scale = 1.0 / math.sqrt(HEAD)
    own_first = seq_index * rows
    groups = [(patch_queries, own_first)]

    def visit(state, query_rows, first, key_heads, value_heads, key_places):

        def refresh(current):
            return update_state(
                current, query_rows, first, key_heads, value_heads, key_places, scale
            )

        return lax.cond(
            key_places[0] <= first + query_rows.shape[0] - 1, refresh, keep_state, state
        )

    initial = tuple(
        (
            (
                jnp.full((heads, query_rows.shape[0]), -1e30, jnp.float32),
                jnp.zeros((heads, query_rows.shape[0]), jnp.float32),
                jnp.zeros((query_rows.shape[0], heads, HEAD), jnp.float32),
            )
            for query_rows, first in groups
        )
    )
    key_piece = lax.all_gather(patch_keys, "seq", axis=0, tiled=True)
    value_piece = lax.all_gather(patch_values, "seq", axis=0, tiled=True)
    count = key_piece.shape[0]
    span = math.gcd(count, 1024)

    def one_span(index, states):
        offset = index * span
        key_heads = lax.dynamic_slice_in_dim(key_piece, offset, span, 0).reshape(span, heads, HEAD)
        value_heads = lax.dynamic_slice_in_dim(value_piece, offset, span, 0).reshape(
            span, heads, HEAD
        )
        key_places = offset + jnp.arange(span, dtype=jnp.int32)
        updated = []
        for (query_rows, first), state in zip(groups, states):
            updated.append(visit(state, query_rows, first, key_heads, value_heads, key_places))
        return tuple(updated)

    states = lax.fori_loop(0, count // span, one_span, initial)
    outputs = [finish_state(state) for state in states]
    attended = outputs[0]
    reduced = lax.psum(jnp.dot(attended, global_down, preferred_element_type=jnp.float32), "row")
    task_scales = select_rows(global_scales, patch_tasks)
    scaled = (reduced * task_scales).astype(jnp.bfloat16)
    mixed = lax.psum_scatter(
        contract(output_weight, attended, 0, 1).astype(jnp.bfloat16),
        "row",
        scatter_dimension=0,
        tiled=True,
    ).astype(jnp.float32)
    mixed = mixed + jnp.transpose(residual.astype(jnp.float32)) + contract(global_up, scaled, 0, 1)
    mixed_b = mixed.astype(jnp.bfloat16)
    own_patches = rows // row_count
    own_bytes = own_patches * PATCH
    rows_in, rows_out = (
        lax.all_gather(hidden_in, "seq", axis=1, tiled=True),
        lax.all_gather(hidden_out, "seq", axis=1, tiled=True),
    )
    partial_value = contract(mixed_b, local_weight, 0, 0)
    projected = lax.psum(partial_value.astype(jnp.bfloat16), "row")
    every = local_inputs(
        byte_ids,
        projected,
        patch_tasks,
        byte_table,
        position_table,
        norm_gain,
        local_down,
        local_scales,
    )
    normed_all = every[2]
    shrunk_all = every[5]
    cotangent_all = lax.all_gather(cotangent, "row", axis=0, tiled=True)
    inputs, inverse, normed, lowered, scales, shrunk, byte_tasks = [
        lax.dynamic_slice_in_dim(value, row_index * own_bytes, own_bytes, 0) for value in every
    ]
    upper = contract(normed_all, rows_in, 1, 1) + jnp.dot(
        shrunk_all, local_up, preferred_element_type=jnp.float32
    )
    through = contract(cotangent_all, rows_out, 1, 1)
    grown = (through * gelu_slope(upper)).astype(jnp.bfloat16)
    grad_local_up = contract(shrunk_all, grown, 0, 0)
    back_norm, back_rank = (
        lax.psum_scatter(
            jnp.dot(grown, rows_in, preferred_element_type=jnp.float32).astype(jnp.bfloat16),
            "row",
            scatter_dimension=0,
            tiled=True,
        ).astype(jnp.float32),
        lax.psum_scatter(
            contract(grown, local_up, 1, 1).astype(jnp.bfloat16),
            "row",
            scatter_dimension=0,
            tiled=True,
        ).astype(jnp.float32),
    )
    grad_local_scales = task_totals(byte_tasks, back_rank * lowered)
    moved = (back_rank * scales).astype(jnp.bfloat16)
    grad_local_down = contract(normed, moved, 0, 0)
    back_total = back_norm + contract(moved, local_down, 1, 1)
    gained = back_total * norm_gain
    average = jnp.mean(gained * inputs, axis=1, keepdims=True)
    back_inputs = cotangent.astype(jnp.float32) + inverse * (
        gained - inputs * inverse * inverse * average
    )
    patch_grad = back_inputs.reshape(own_patches, PATCH, -1).sum(axis=1).astype(jnp.bfloat16)
    back_mixed = contract(
        lax.all_gather(patch_grad, "row", axis=0, tiled=True), local_weight, 1, 1
    ).astype(jnp.bfloat16)
    grad_global_up = contract(scaled, back_mixed, 0, 0)
    back_scaled = lax.psum(contract(back_mixed, global_up, 1, 1), "row")
    grad_global_scales = task_totals(patch_tasks, back_scaled * reduced)
    back_reduced = (back_scaled * task_scales).astype(jnp.bfloat16)
    grad_global_down = contract(attended, back_reduced, 0, 0)
    grad_global_down, grad_global_up, grad_global_scales, grad_local_up = lax.psum(
        (grad_global_down, grad_global_up, grad_global_scales, grad_local_up), "seq"
    )
    grad_local_down, grad_local_scales = lax.psum(
        (grad_local_down, grad_local_scales), ("seq", "row")
    )
    return (
        grad_global_down,
        grad_global_up,
        grad_global_scales,
        grad_local_down,
        grad_local_up,
        grad_local_scales,
    )


MESH = pl.DeviceIdType.MESH


def remote(src, dst, send, recv, seq, row):
    return pltpu.make_async_remote_copy(
        src_ref=src,
        dst_ref=dst,
        send_sem=send,
        recv_sem=recv,
        device_id=(seq, row),
        device_id_type=MESH,
    )


def greet(peers):
    barrier = pltpu.get_barrier_semaphore()
    for seq, row in peers:
        pl.semaphore_signal(barrier, inc=1, device_id=(seq, row), device_id_type=MESH)
    pl.semaphore_wait(barrier, len(peers))


def front_kernel(
    chips, depth, q_ref, k_ref, v_ref, hi_ref, ho_ref, cot_ref, ow_hbm, lw_ref, gd_ref, gu_ref,
    res_ref, att_out, proj_out, m_out, hi_out, ho_out, cot_out,
    ow_ref, ow_sem, qb, kb, vb, ob, att, wb, cotb, lwb, w2, acc, e1, e1r, mb, mr,
    a_send, a_recv, f_send, f_recv, o_send, o_recv, z_send, z_recv, x_send, x_recv,
    p_send, p_recv, c_send, c_recv, y_send, y_recv,
):
    me = lax.axis_index("seq")
    row = lax.axis_index("row")
    other = 1 - row
    chip, core = me // 2, lax.rem(me, 2)
    mate = 2 * chip + (1 - core)
    rows = q_ref.shape[0]
    half = lw_ref.shape[0] // 2

    def at(number):
        return lax.rem(number + 2 * chips, chips)

    def heads_of(number):
        return pl.ds(pl.multiple_of(number * HEAD, HEAD), HEAD)

    ow_copy = pltpu.make_async_copy(ow_hbm, ow_ref, ow_sem)
    ow_copy.start()
    shard = hi_ref.shape[0]
    wb[me, :shard] = hi_ref[...]
    wb[me, shard:] = ho_ref[...]
    greet([(2 * at(chip + d) + core, row) for d in range(1, chips)] + [(mate, row), (me, other)])

    own = heads_of(chip)
    sends = []
    arrivals = {}
    own_half = pl.ds(pl.multiple_of(core * half, half), half)
    mate_half = pl.ds(pl.multiple_of((1 - core) * half, half), half)
    lw_copy = remote(lw_ref.at[own_half], lwb.at[own_half], y_send.at[0], y_recv.at[0], me, other)
    lw_copy.start()
    forwards = {}
    order = sorted(range(1, chips), key=lambda d: -min(d, chips - d))
    for d in order:
        to = at(chip + d)
        for which, (src, dst) in enumerate(
            ((k_ref, kb.at[me]), (v_ref, vb.at[me]), (q_ref, qb.at[chip]))
        ):
            copy = remote(
                src.at[:, heads_of(to)], dst, a_send.at[which, d], a_recv.at[which, d],
                2 * to + core, row,
            )
            copy.start()
            arrivals[which, d] = copy
    for which, (src, dst) in enumerate(((k_ref, kb), (v_ref, vb))):
        copy = remote(
            src.at[:, own], dst.at[me], f_send.at[which, 0], f_recv.at[which, 0], mate, row
        )
        copy.start()
        forwards[which, 0] = copy
    cot_copy = remote(cot_ref, cotb, c_send.at[0], c_recv.at[0], me, other)
    cot_copy.start()

    levels = chips // depth
    level, side = chip // depth, lax.rem(chip, depth)
    z_copies = []
    for d in range(1, levels):
        to = lax.rem(level + d, levels) * depth + side
        copy = remote(wb.at[me], wb.at[me], z_send.at[d], z_recv.at[d], 2 * to + core, row)
        copy.start()
        z_copies.append((d, copy))
    neighbour = 2 * (level * depth + (1 - side)) + core
    x_copies = []
    p_copies = []

    def pass_side(d, src, slot):
        copy = remote(src, wb.at[slot], x_send.at[d], x_recv.at[d], neighbour, row)
        copy.start()
        x_copies.append((d, copy))

    def pass_mate(number, src, slot):
        copy = remote(src, wb.at[slot], p_send.at[number], p_recv.at[number], mate, row)
        copy.start()
        p_copies.append(copy)

    pass_side(0, wb.at[me], me)
    pass_mate(0, wb.at[me], me)

    qb[chip] = q_ref[:, own]
    kb[me] = k_ref[:, own]
    vb[me] = v_ref[:, own]

    mb[...] = jnp.dot(
        gu_ref[...], lw_ref[...], preferred_element_type=jnp.float32
    ).astype(jnp.bfloat16)
    m_copy = remote(mb, mr, y_send.at[2], y_recv.at[2], me, other)
    m_copy.start()

    width = lw_ref.shape[0]
    tile = math.gcd(ow_ref.shape[0], 256)
    columns = lw_ref.shape[1]

    ow_copy.wait()

    @pl.loop(0, ow_ref.shape[0] // tile)
    def _(index):
        part = pl.ds(pl.multiple_of(index * tile, tile), tile)
        acc[part] = jnp.dot(
            ow_ref[part, pl.ds(pl.multiple_of(row * width, width), width)],
            lw_ref[...],
            preferred_element_type=jnp.float32,
        )

    lw_copy.wait_recv()
    lw_mate = remote(lwb.at[own_half], lwb.at[own_half], y_send.at[1], y_recv.at[1], mate, row)
    lw_mate.start()
    lw_mate.wait_recv()

    @pl.loop(0, ow_ref.shape[0] // tile)
    def _(index):
        part = pl.ds(pl.multiple_of(index * tile, tile), tile)
        total = acc[part] + jnp.dot(
            ow_ref[part, pl.ds(pl.multiple_of(other * width, width), width)],
            lwb[...],
            preferred_element_type=jnp.float32,
        )
        w2[part] = total.astype(jnp.bfloat16)

    for d in reversed(range(1, chips)):
        for which, buffer in ((0, kb), (1, vb)):
            arrivals[which, d].wait_recv()
            slot = 2 * at(chip - d) + core
            copy = remote(
                buffer.at[slot], buffer.at[slot], f_send.at[which, d], f_recv.at[which, d],
                mate, row,
            )
            copy.start()
            forwards[which, d] = copy
        arrivals[2, d].wait_recv()
    for copy in forwards.values():
        copy.wait_recv()

    scale = 1.0 / math.sqrt(HEAD)
    for i in reversed(range(chips)):
        span = (2 * i + 2) * rows
        keys = kb[: 2 * i + 2].reshape(span, HEAD)
        values = vb[: 2 * i + 2].reshape(span, HEAD)
        scores = contract(qb[i], keys, 1, 1) * scale
        last = 2 * rows
        places = lax.broadcasted_iota(jnp.int32, (rows, span), 1)
        queries = lax.broadcasted_iota(jnp.int32, (rows, span), 0) + (2 * i + core) * rows
        scores = jnp.where(places <= queries, scores, -1e30)
        top = jnp.max(scores, axis=1, keepdims=True)
        weights = jnp.exp(scores - top)
        mass = jnp.sum(weights, axis=1, keepdims=True)
        mixed = jnp.dot(weights.astype(jnp.bfloat16), values, preferred_element_type=jnp.float32)
        ob[i] = (mixed / mass).astype(jnp.bfloat16)

        @pl.when(i != chip)
        def _():
            remote(
                ob.at[i], att.at[:, own], o_send.at[i], o_recv.at[chip], 2 * i + core, row
            ).start()

        @pl.when(i == chip)
        def _():
            att[:, own] = ob[i]

    for d, copy in z_copies:
        copy.wait_recv()
        slot = 2 * (lax.rem(level - d + levels, levels) * depth + side) + core
        pass_side(d, wb.at[slot], slot)
        pass_mate(d, wb.at[slot], slot)
    for d, copy in list(x_copies):
        copy.wait_recv()
        slot = 2 * (lax.rem(level - d + levels, levels) * depth + (1 - side)) + core
        pass_mate(levels + d, wb.at[slot], slot)

    for i in range(chips):

        @pl.when(i != chip)
        def _():
            back = remote(
                ob.at[i], att.at[:, heads_of(i)], o_send.at[i], o_recv.at[i], 2 * i + core, row
            )
            back.wait_recv()
            back.wait_send()

    value = jnp.dot(att[...], w2[...], preferred_element_type=jnp.float32)
    e1[:, :columns] = (
        value
        + jnp.dot(res_ref[...], lw_ref[...], preferred_element_type=jnp.float32)
    ).astype(jnp.bfloat16)
    e1[:, columns:] = jnp.zeros((rows, e1.shape[1] - columns), jnp.bfloat16)
    e1[:, columns : columns + gd_ref.shape[0]] = contract(att[...], gd_ref[...], 1, 1).astype(
        jnp.bfloat16
    )
    e_copy = remote(e1, e1r, y_send.at[3], y_recv.at[3], me, other)
    e_copy.start()
    att_out[...] = att[...]
    cot_copy.wait_recv()
    cot_out[row] = cot_ref[...]
    cot_out[other] = cotb[...]
    m_copy.wait_recv()
    m_out[...] = mb[...].astype(jnp.float32) + mr[...].astype(jnp.float32)
    for copy in p_copies:
        copy.wait_recv()
    hi_out[...] = wb[:, :shard]
    ho_out[...] = wb[:, shard:]
    e_copy.wait_recv()
    proj_out[...] = e1[...].astype(jnp.float32) + e1r[...].astype(jnp.float32)
    for copy in (
        [lw_copy, lw_mate, cot_copy, m_copy, e_copy]
        + list(arrivals.values())
        + list(forwards.values())
        + [copy for d, copy in z_copies + x_copies]
        + p_copies
    ):
        copy.wait_send()


def front(q, k, v, hi, ho, cot, ow, lw, gd, gu, res, count):
    chips = q.shape[1] // HEAD
    rows = q.shape[0]
    depth = 2
    levels = chips // depth
    columns = lw.shape[1]
    wide = columns + HEAD
    vm = pl.BlockSpec(memory_space=pltpu.VMEM)
    dma = pltpu.SemaphoreType.DMA
    bf, f32 = jnp.bfloat16, jnp.float32
    return pl.pallas_call(
        functools.partial(front_kernel, chips, depth),
        out_shape=(
            jax.ShapeDtypeStruct(q.shape, bf),
            jax.ShapeDtypeStruct((rows, wide), f32),
            jax.ShapeDtypeStruct((gu.shape[0], columns), f32),
            jax.ShapeDtypeStruct((count,) + hi.shape, bf),
            jax.ShapeDtypeStruct((count,) + ho.shape, bf),
            jax.ShapeDtypeStruct((2,) + cot.shape, bf),
        ),
        in_specs=[vm] * 6 + [pl.BlockSpec(memory_space=pl.ANY)] + [vm] * 4,
        out_specs=(vm,) * 6,
        scratch_shapes=[
            pltpu.VMEM(ow.shape, bf),
            dma,
            pltpu.VMEM((chips, rows, HEAD), bf),
            pltpu.VMEM((count, rows, HEAD), bf),
            pltpu.VMEM((count, rows, HEAD), bf),
            pltpu.VMEM((chips, rows, HEAD), bf),
            pltpu.VMEM(q.shape, bf),
            pltpu.VMEM((count, 2 * hi.shape[0], hi.shape[1]), bf),
            pltpu.VMEM(cot.shape, bf),
            pltpu.VMEM(lw.shape, bf),
            pltpu.VMEM((ow.shape[0], columns), bf),
            pltpu.VMEM((ow.shape[0], columns), f32),
            pltpu.VMEM((rows, wide), bf),
            pltpu.VMEM((rows, wide), bf),
            pltpu.VMEM((gu.shape[0], columns), bf),
            pltpu.VMEM((gu.shape[0], columns), bf),
            dma((3, chips)), dma((3, chips)),
            dma((2, chips)), dma((2, chips)),
            dma((chips,)), dma((chips,)),
            dma((levels,)), dma((levels,)),
            dma((levels,)), dma((levels,)),
            dma((chips,)), dma((chips,)),
            dma((1,)), dma((1,)),
            dma((4,)), dma((4,)),
        ],
        compiler_params=pltpu.CompilerParams(
            collective_id=0, has_side_effects=True, vmem_limit_bytes=60 * 1024 * 1024
        ),
        name="front",
    )(q, k, v, hi, ho, cot, ow, lw, gd, gu, res)


def swap_kernel(x_ref, o_ref, buf, send, recv):
    me, row = lax.axis_index("seq"), lax.axis_index("row")
    greet([(me, 1 - row)])
    copy = remote(x_ref, buf, send, recv, me, 1 - row)
    copy.start()
    copy.wait()
    o_ref[...] = x_ref[...].astype(jnp.float32) + buf[...].astype(jnp.float32)


def row_sum(x):
    vm = pl.BlockSpec(memory_space=pltpu.VMEM)
    return pl.pallas_call(
        swap_kernel,
        out_shape=jax.ShapeDtypeStruct(x.shape, jnp.float32),
        in_specs=[vm],
        out_specs=vm,
        scratch_shapes=[
            pltpu.VMEM(x.shape, x.dtype), pltpu.SemaphoreType.DMA, pltpu.SemaphoreType.DMA
        ],
        compiler_params=pltpu.CompilerParams(collective_id=1, has_side_effects=True),
        name="row_sum",
    )(x)


def total_kernel(count, shared, g_ref, o_ref, part, result, full, s1, r1, s2, r2, s3, r3):
    me, row = lax.axis_index("seq"), lax.axis_index("row")
    other = 1 - row
    peers = [(lax.rem(me + d, count), row) for d in range(1, count)]
    cross = [(lax.rem(me + d, count), other) for d in range(count)]
    greet(peers + cross)
    first = []
    for d in range(1, count):
        to = lax.rem(me + d, count)
        copy = remote(g_ref.at[to], part.at[row, me], s1.at[d], r1.at[d], to, row)
        copy.start()
        first.append(copy)
    crossing = []
    for index, to in enumerate(shared):
        copy = remote(g_ref.at[to], part.at[row, me], s3.at[index], r3.at[me], to, other)
        copy.start()
        crossing.append(copy)
    part[row, me] = g_ref[me]
    for copy in first:
        copy.wait_recv()

    def add(side):
        return jnp.sum(part[side].astype(jnp.float32), axis=0)

    result[...] = add(row).astype(jnp.bfloat16)

    @pl.when(me >= shared[0])
    def _():
        for source in range(count):
            remote(
                g_ref.at[0], part.at[other, source], s3.at[0], r3.at[source], me, other
            ).wait_recv()
        result[...] = (add(0) + add(1)).astype(jnp.bfloat16)

    second = []
    for d in range(1, count):
        to = lax.rem(me + d, count)
        copy = remote(result, full.at[me], s2.at[d], r2.at[d], to, row)
        copy.start()
        second.append(copy)
    full[me] = result[...]
    for copy in second:
        copy.wait_recv()
    o_ref[...] = full[...].astype(jnp.float32)
    for copy in first + crossing + second:
        copy.wait_send()


def grand_total(g, shared):
    count = g.shape[0]
    vm = pl.BlockSpec(memory_space=pltpu.VMEM)
    dma = pltpu.SemaphoreType.DMA
    return pl.pallas_call(
        functools.partial(total_kernel, count, shared),
        out_shape=jax.ShapeDtypeStruct(g.shape, jnp.float32),
        in_specs=[vm],
        out_specs=vm,
        scratch_shapes=[
            pltpu.VMEM((2,) + g.shape, g.dtype),
            pltpu.VMEM(g.shape[1:], g.dtype),
            pltpu.VMEM(g.shape, g.dtype),
            dma((count,)), dma((count,)),
            dma((count,)), dma((count,)),
            dma((len(shared),)), dma((count,)),
        ],
        compiler_params=pltpu.CompilerParams(collective_id=2, has_side_effects=True),
        name="grand_total",
    )(g)


def paired_body(
    patch_queries,
    patch_keys,
    patch_values,
    patch_tasks,
    residual,
    output_weight,
    global_down,
    global_up,
    global_scales,
    local_weight,
    byte_ids,
    byte_table,
    position_table,
    norm_gain,
    hidden_in,
    hidden_out,
    local_down,
    local_up,
    local_scales,
    cotangent,
):
    count = lax.axis_size("seq")
    bf = jnp.bfloat16
    rank = global_up.shape[0]
    columns = local_weight.shape[1]
    hidden = hidden_in.shape[0]
    attended, proj, bridge, rows_in, rows_out, cot = front(
        patch_queries, patch_keys, patch_values, jnp.transpose(hidden_in),
        jnp.transpose(hidden_out), cotangent, output_weight, local_weight,
        jnp.transpose(global_down), global_up, residual, count,
    )
    reduced = proj[:, columns : columns + rank]
    rows_in = rows_in.reshape(columns, hidden)
    rows_out = rows_out.reshape(columns, hidden)
    cot = cot.reshape(-1, columns)
    task_scales = select_rows(global_scales, patch_tasks)
    scaled = (reduced * task_scales).astype(bf)
    bridge_b = bridge.astype(bf)
    projected = (
        proj[:, :columns] + jnp.dot(scaled, bridge_b, preferred_element_type=jnp.float32)
    ).astype(bf)
    inputs, inverse, normed, lowered, scales, shrunk, byte_tasks = local_inputs(
        byte_ids, projected, patch_tasks, byte_table, position_table, norm_gain, local_down,
        local_scales,
    )
    upper = jnp.dot(normed, rows_in, preferred_element_type=jnp.float32) + jnp.dot(
        shrunk, local_up, preferred_element_type=jnp.float32
    )
    through = jnp.dot(cot, rows_out, preferred_element_type=jnp.float32)
    grown = (through * gelu_slope(upper)).astype(bf)
    grad_local_up = contract(shrunk, grown, 0, 0)
    back_rank = contract(grown, local_up, 1, 1)
    moved = (back_rank * scales).astype(bf)
    grad_local_scales = task_totals(byte_tasks, back_rank * lowered)
    grad_local_down = contract(moved, normed, 0, 0)
    back_total = contract(grown, rows_in, 1, 1) + contract(moved, local_down, 1, 1)
    gained = back_total * norm_gain
    average = jnp.mean(gained * inputs, axis=1, keepdims=True)
    back_inputs = inverse * (gained - inputs * inverse * inverse * average)
    patches = patch_tasks.shape[0]
    back_part = back_inputs.reshape(patches, PATCH, -1).sum(axis=1).astype(bf)
    cot_sum = cot.astype(jnp.float32).reshape(patches, PATCH, -1).sum(axis=1)
    patch_grad = (row_sum(back_part) + cot_sum).astype(bf)
    back_mixed = contract(patch_grad, local_weight, 1, 1).astype(bf)
    grad_global_up = contract(scaled, back_mixed, 0, 0)
    back_scaled = contract(patch_grad, bridge_b, 1, 1)
    grad_global_scales = task_totals(patch_tasks, back_scaled * reduced)
    back_reduced = (back_scaled * task_scales).astype(bf)
    grad_global_down = contract(back_reduced, attended, 0, 0)

    spare = hidden - columns - rank
    small = jnp.concatenate([0.5 * grad_global_scales, grad_local_scales], axis=0)
    last = jnp.concatenate(
        [grad_local_down, small, jnp.zeros((rank, spare), jnp.float32)], axis=1
    )
    packed = jnp.concatenate(
        [grad_global_down, grad_global_up, grad_local_up, last], axis=0
    ).astype(bf)
    blocks = packed.reshape(count, 16, -1)
    shared = tuple(range(count - count // 4, count))
    summed = grand_total(blocks, shared).reshape(packed.shape)
    last = summed[3 * rank :]
    return (
        jnp.transpose(summed[:rank]),
        summed[rank : 2 * rank],
        last[:TASKS, columns : columns + rank],
        jnp.transpose(last[:, :columns]),
        summed[2 * rank : 3 * rank],
        last[TASKS:, columns : columns + rank],
    )


def pick_body(seq_count, row_count, *args):
    heads = args[0].shape[1] // HEAD
    rank = args[7].shape[0]
    hidden = args[14].shape[0]
    fits = (
        row_count == 2
        and seq_count == 2 * heads
        and heads % 4 == 0
        and rank == 2 * TASKS
        and args[0].shape[1] == hidden
        and (4 * rank * hidden) % (seq_count * 16 * HEAD) == 0
        and hidden >= args[9].shape[1] + rank
    )
    return paired_body(*args) if fits else general_body(*args)


def solution(mesh):
    placed = (
        P("seq", "row"),
        P("seq", "row"),
        P("seq", "row"),
        P("seq"),
        P("seq", "row"),
        P("row", None),
        P("row", None),
        P(None, "row"),
        P(),
        P("row", None),
        P("seq"),
        P(),
        P(),
        P(),
        P("row", "seq"),
        P("row", "seq"),
        P(),
        P(None, "row"),
        P(),
        P(("seq", "row"), None),
    )
    chosen = functools.partial(pick_body, mesh.shape["seq"], mesh.shape["row"])
    return jax.shard_map(
        chosen,
        mesh=mesh,
        in_specs=placed,
        out_specs=(P("row", None), P(None, "row"), P(), P(), P(None, "row"), P()),
        check_vma=False,
    )
```

profile of v0, /device:TPU:0, one launch (start us, length us, event | category | flops | bytes accessed | tf_op | source)
XLA Modules:
  0.0 112.5 jit_solution(15649797082843941057)
XLA Ops:
  0.6 0.9 fusion.19
  1.6 0.8 convert_element_type.56
  2.5 0.7 eq.23
  3.3 1.2 %fusion.12 = f32[1024,16]{0,1:T(8,128)S(1)} fusion(f32[8,16]{1,0:T(8,128)} %param.38, s32[1024]{0:T(1024)S(1)} %eq.26), kind=kOutput, calls=%fused_computation.30 | convolution fusion | flops 1581056 | bytes 70144 | tf_op jit(solution)/shard_map/dot_general | solution.py:27
  4.4 54.0 %front.1 = (bf16[128,1024]{1,0:T(8,128)(2,1)}, f32[128,640]{1,0:T(8,128)}, f32[16,512]{1,0:T(8,128)}, bf16[16,32,1024]{2,1,0:T(8,128)(2,1)}, bf16[16,32,1024]{2,...) custom-call(bf16[128,1024]{1,0:T(8,128)(2,1)} %q_ref.1, bf16[128,1024]{1,0:T(8,128)(2,1)} %k_ref.1, bf16[128,1024]{1,0:T(8,128)(2,1)} %v_ref.1, ...), custom_call_target="tpu_custom_call" | custom-call | tf_op jit(solution)/shard_map/front/pallas_call | solution.py:509
  58.4 0.9 multiply_convert_fusion.3
  59.3 1.9 %convert_reduce_fusion = f32[128,512]{1,0:T(8,128)S(1)} fusion(bf16[128,8,512]{2,1,0:T(8,128)(2,1)} %bitcast.46), kind=kLoop, calls=%fused_computation.7 | loop fusion | flops 983040 | bytes 1310720 | tf_op jit(solution)/shard_map/reduce_sum | solution.py:710
  61.2 1.1 %fusion.8 = f32[128,512]{1,0:T(8,128)S(1)} fusion(bf16[128,16]{1,0:T(8,128)(2,1)S(1)} %multiply_convert_fusion.3, f32[128,640]{1,0:T(8,128)} %get-tuple-element.12, f32[16,512]{1,0:T(8,128)} %get-tuple-element.13), kind=kOutput, calls=%fused_computation.19 | convolution fusion | flops 2301952 | bytes 561152 | tf_op jit(solution)/shard_map/dot_general | solution.py:688
  62.4 0.6 multiply_reduce_fusion.1
  64.6 1.2 %fusion.28 = f32[1024,1024]{1,0:T(8,128)S(1)} fusion(bf16[1024,512]{1,0:T(8,128)(2,1)S(1)} %bitcast.47, bf16[512,1024]{1,0:T(8,128)(2,1)S(1)} %bitcast.54), kind=kOutput, calls=%fused_computation.55 | convolution fusion | flops 1073741824 | bytes 6291456 | tf_op jit(solution)/shard_map/dot_general | solution.py:697
  65.9 1.3 %fusion.29 = f32[1024,1024]{1,0:T(8,128)S(1)} fusion(bf16[1024,512]{1,0:T(8,128)(2,1)S(1)} %multiply_convert_fusion, bf16[512,1024]{1,0:T(8,128)(2,1)S(1)} %bitcast.52), kind=kOutput, calls=%fused_computation.56 | convolution fusion | flops 1073741824 | bytes 6291456 | tf_op jit(solution)/shard_map/dot_general | solution.py:694
  67.2 2.3 %fusion.5 = bf16[1024,1024]{1,0:T(8,128)(2,1)S(1)} fusion(f32[1024,1024]{1,0:T(8,128)S(1)} %fusion.28, f32[1024,1024]{1,0:T(8,128)S(1)} %fusion.29, bf16[1024,16]{0,1:T(8,128)(2,1)S(1)} %get-tuple-element.26, bf16[16,1024]{1,0:T(8,128)(2,1)S(1)} %copy-done.6), kind=kOutput, calls=%fused_computation.6 | convolution fusion | flops 45088768 | bytes 10551296 | tf_op jit(solution)/shard_map/dot_general | solution.py:694
  69.8 0.7 multiply_convert_fusion.1
  70.5 1.3 %fusion.30 = f32[1024,512]{1,0:T(8,128)S(1)} fusion(bf16[1024,1024]{1,0:T(8,128)(2,1)S(1)} %fusion.5, bf16[512,1024]{1,0:T(8,128)(2,1)S(1)} %bitcast.53), kind=kOutput, calls=%fused_computation.57 | convolution fusion | flops 1073741824 | bytes 5242880 | tf_op jit(solution)/shard_map/dot_general | solution.py:18
  73.3 1.6 %bitcast_reduce_fusion.x_ref = bf16[128,512]{1,0:T(8,128)(2,1)} fusion(f32[1024,512]{1,0:T(8,128)S(1)} %get-tuple-element.31, f32[1024,512]{1,0:T(8,128)S(1)} %get-tuple-element.25, f32[1024]{0:T(1024)S(1)} %broadcast_multiply_fusion, f32[1024]{0:T(1024)S(1)} %add_rsqrt_fusion), kind=kLoop, calls=%fused_computation.8 | loop fusion | flops 3080192 | bytes 4333568 | tf_op jit(solution)/shard_map/reduce_sum | solution.py:709
  74.8 6.6 %row_sum.1 = f32[128,512]{1,0:T(8,128)} custom-call(bf16[128,512]{1,0:T(8,128)(2,1)} %bitcast_reduce_fusion.x_ref), custom_call_target="tpu_custom_call" | custom-call | tf_op jit(solution)/shard_map/row_sum/pallas_call | solution.py:565
  81.5 1.0 add_convert_fusion
  83.5 1.1 fusion.10
  84.7 0.7 convert_element_type.71.g_ref
  85.4 22.9 %grand_total.1 = f32[16,16,256]{2,1,0:T(8,128)} custom-call(bf16[16,16,256]{2,1,0:T(8,128)(2,1)} %convert_element_type.71.g_ref), custom_call_target="tpu_custom_call" | custom-call | tf_op jit(solution)/shard_map/grand_total/pallas_call | solution.py:630
  108.4 1.0 fusion.26
  109.3 0.6 slice.50
  111.2 0.6 slice.44
  111.8 0.6 slice.42
  (43 shorter events, 5.9 us)
Async XLA Ops:
  0.6 61.7 %copy-start = (bf16[256,512]{1,0:T(8,128)(2,1)S(1)}, bf16[256,512]{1,0:T(8,128)(2,1)}, u32[]{:S(2)}) copy-start(bf16[256,512]{1,0:T(8,128)(2,1)} %param.31) | copy-start | bytes 786436
  4.4 57.9 %copy-start.11 = (s32[1024]{0:T(1024)S(1)}, s32[1024]{0:T(1024)}, u32[]{:S(2)}) copy-start(s32[1024]{0:T(1024)} %param.30) | copy-start | bytes 12292
  61.2 1.8 %copy-start.7 = (f32[512]{0:T(512)S(1)}, f32[512]{0:T(512)}, u32[]{:S(2)}) copy-start(f32[512]{0:T(512)} %param.33) | copy-start | bytes 6148
  63.0 0.7 copy-start.5
  63.1 1.2 %copy-start.2 = (bf16[2,512,512]{2,1,0:T(8,128)(2,1)S(1)}, bf16[2,512,512]{2,1,0:T(8,128)(2,1)}, u32[]{:S(2)}) copy-start(bf16[2,512,512]{2,1,0:T(8,128)(2,1)} %get-tuple-element.14) | copy-start | bytes 3145732
  63.1 1.5 %copy-start.10 = (bf16[16,32,1024]{2,1,0:T(8,128)(2,1)S(1)}, bf16[16,32,1024]{2,1,0:T(8,128)(2,1)}, u32[]{:S(2)}) copy-start(bf16[16,32,1024]{2,1,0:T(8,128)(2,1)} %get-tuple-element.15) | copy-start | bytes 3145732
  64.6 1.3 %copy-start.9 = (bf16[16,32,1024]{2,1,0:T(8,128)(2,1)S(1)}, bf16[16,32,1024]{2,1,0:T(8,128)(2,1)}, u32[]{:S(2)}) copy-start(bf16[16,32,1024]{2,1,0:T(8,128)(2,1)} %get-tuple-element.16) | copy-start | bytes 3145732
  65.9 1.3 %copy-start.6 = (bf16[16,1024]{1,0:T(8,128)(2,1)S(1)}, bf16[16,1024]{1,0:T(8,128)(2,1)}, u32[]{:S(2)}) copy-start(bf16[16,1024]{1,0:T(8,128)(2,1)} %param.37) | copy-start | bytes 98308
  73.2 9.2 %copy-start.4 = (f32[16,512]{1,0:T(8,128)S(1)}, f32[16,512]{1,0:T(8,128)}, u32[]{:S(2)}) copy-start(f32[16,512]{1,0:T(8,128)} %get-tuple-element.13) | copy-start | bytes 98308
  73.3 9.4 %copy-start.3 = (bf16[128,1024]{1,0:T(8,128)(2,1)S(1)}, bf16[128,1024]{1,0:T(8,128)(2,1)}, u32[]{:S(2)}) copy-start(bf16[128,1024]{1,0:T(8,128)(2,1)} %get-tuple-element.17) | copy-start | bytes 786436
  73.3 9.5 %copy-start.1 = (bf16[1024,512]{1,0:T(8,128)(2,1)S(1)}, bf16[1024,512]{1,0:T(8,128)(2,1)}, u32[]{:S(2)}) copy-start(bf16[1024,512]{1,0:T(8,128)(2,1)} %lw_ref.1) | copy-start | bytes 3145732
  74.8 8.6 %copy-start.8 = (s32[128]{0:T(128)S(1)}, s32[128]{0:T(128)}, u32[]{:S(2)}) copy-start(s32[128]{0:T(128)} %param.23) | copy-start | bytes 1540
where the time goes:
time: 113 us; the launch traced here: 112 us
  Pallas kernels  83.5 us (74%)
  matrix products  14.8 us (13%)
  local copies, waits for them, and re-layouts  6.86 us (6%)
  other arithmetic  6.43 us (6%)
    pallas_call x1, Pallas kernels, front(): pl.pallas_call(functools.partial(front_kernel, chips, depth), out_shape=(...  54 us
    pallas_call x1, Pallas kernels, grand_total(): pl.pallas_call(functools.partial(total_kernel, count, shared), out_shape=...  22.9 us
    pallas_call x1, Pallas kernels, row_sum(): pl.pallas_call(swap_kernel, out_shape=jax.ShapeDtypeStruct(x.shape, jnp.f...  6.63 us
    dot_general x8, matrix products, contract(): lax.dot_general(left, right, (((left_dim,), (right_dim,)), ((), ())), pre...  4.12 us

commit v1 on v0

v1 whole, which is shorter than its diff:
```python
import functools
import math

import jax
import jax.numpy as jnp
from jax import lax
from jax.experimental import pallas as pl
from jax.experimental.pallas import tpu as pltpu
from jax.sharding import PartitionSpec as P

HEAD = 128
VOCAB = 256
PATCH = 8
TASKS = 8


def contract(left, right, left_dim, right_dim):
    return lax.dot_general(
        left, right, (((left_dim,), (right_dim,)), ((), ())), preferred_element_type=jnp.float32
    )


def select_rows(table, tasks):
    picks = (tasks[:, None] == jnp.arange(table.shape[0], dtype=jnp.int32)[None, :]).astype(
        jnp.float32
    )
    return jnp.dot(picks, table, precision=lax.Precision.HIGHEST)


def task_totals(tasks, values):
    picks = (tasks[:, None] == jnp.arange(TASKS, dtype=jnp.int32)[None, :]).astype(jnp.float32)
    return lax.dot_general(picks, values, (((0,), (0,)), ((), ())), precision=lax.Precision.HIGHEST)


def gelu_slope(upper):
    cumulative = 0.5 * (1.0 + lax.erf(upper * 0.7071067811865476))
    density = jnp.exp(-0.5 * upper * upper) * 0.3989422804014327
    return cumulative + upper * density


def local_inputs(
    identities, projected, tasks, byte_table, position_table, norm_gain, local_down, local_scales
):
    count = identities.shape[0]
    picks = (identities[:, None] == jnp.arange(VOCAB, dtype=jnp.int32)[None, :]).astype(
        jnp.bfloat16
    )
    embedded = jnp.dot(picks, byte_table, preferred_element_type=jnp.float32)
    patches = count // PATCH
    inputs = (
        embedded.reshape(patches, PATCH, -1)
        + position_table.astype(jnp.float32)[None]
        + projected.astype(jnp.float32)[:, None, :]
    )
    inputs = inputs.reshape(count, -1)
    inverse = lax.rsqrt(jnp.mean(inputs * inputs, axis=1, keepdims=True) + 1e-06)
    normed = (inputs * inverse * norm_gain).astype(jnp.bfloat16)
    lowered = jnp.dot(normed, local_down, preferred_element_type=jnp.float32)
    byte_tasks = jnp.repeat(tasks, PATCH)
    scales = select_rows(local_scales, byte_tasks)
    shrunk = (lowered * scales).astype(jnp.bfloat16)
    return (inputs, inverse, normed, lowered, scales, shrunk, byte_tasks)


def keep_state(current):
    return current


def update_state(state, query_rows, first, key_heads, value_heads, key_places, scale):
    running_max, running_sum, running_out = state
    count = query_rows.shape[0]
    heads = key_heads.shape[1]
    query_heads = query_rows.reshape(count, heads, HEAD)
    scores = (
        jnp.einsum("qhd,khd->hqk", query_heads, key_heads, preferred_element_type=jnp.float32)
        * scale
    )
    query_places = first + jnp.arange(count, dtype=jnp.int32)
    allowed = key_places[None, :] <= query_places[:, None]
    scores = jnp.where(allowed[None], scores, -1e30)
    new_max = jnp.maximum(running_max, jnp.max(scores, axis=2))
    weights = jnp.where(allowed[None], jnp.exp(scores - new_max[:, :, None]), 0.0)
    shrink = jnp.exp(running_max - new_max)
    running_sum = running_sum * shrink + jnp.sum(weights, axis=2)
    mixed = jnp.einsum(
        "hqk,khd->qhd",
        weights.astype(jnp.bfloat16),
        value_heads,
        preferred_element_type=jnp.float32,
    )
    running_out = running_out * jnp.transpose(shrink)[:, :, None] + mixed
    return (new_max, running_sum, running_out)


def finish_state(state):
    running_max, running_sum, running_out = state
    result = running_out / jnp.transpose(running_sum)[:, :, None]
    return result.reshape(result.shape[0], -1).astype(jnp.bfloat16)


def general_body(
    patch_queries,
    patch_keys,
    patch_values,
    patch_tasks,
    residual,
    output_weight,
    global_down,
    global_up,
    global_scales,
    local_weight,
    byte_ids,
    byte_table,
    position_table,
    norm_gain,
    hidden_in,
    hidden_out,
    local_down,
    local_up,
    local_scales,
    cotangent,
):
    rows = patch_queries.shape[0]
    width = patch_queries.shape[1]
    heads = width // HEAD
    row_count = lax.axis_size("row")
    seq_index = lax.axis_index("seq")
    row_index = lax.axis_index("row")
    scale = 1.0 / math.sqrt(HEAD)
    own_first = seq_index * rows
    groups = [(patch_queries, own_first)]

    def visit(state, query_rows, first, key_heads, value_heads, key_places):

        def refresh(current):
            return update_state(
                current, query_rows, first, key_heads, value_heads, key_places, scale
            )

        return lax.cond(
            key_places[0] <= first + query_rows.shape[0] - 1, refresh, keep_state, state
        )

    initial = tuple(
        (
            (
                jnp.full((heads, query_rows.shape[0]), -1e30, jnp.float32),
                jnp.zeros((heads, query_rows.shape[0]), jnp.float32),
                jnp.zeros((query_rows.shape[0], heads, HEAD), jnp.float32),
            )
            for query_rows, first in groups
        )
    )
    key_piece = lax.all_gather(patch_keys, "seq", axis=0, tiled=True)
    value_piece = lax.all_gather(patch_values, "seq", axis=0, tiled=True)
    count = key_piece.shape[0]
    span = math.gcd(count, 1024)

    def one_span(index, states):
        offset = index * span
        key_heads = lax.dynamic_slice_in_dim(key_piece, offset, span, 0).reshape(span, heads, HEAD)
        value_heads = lax.dynamic_slice_in_dim(value_piece, offset, span, 0).reshape(
            span, heads, HEAD
        )
        key_places = offset + jnp.arange(span, dtype=jnp.int32)
        updated = []
        for (query_rows, first), state in zip(groups, states):
            updated.append(visit(state, query_rows, first, key_heads, value_heads, key_places))
        return tuple(updated)

    states = lax.fori_loop(0, count // span, one_span, initial)
    outputs = [finish_state(state) for state in states]
    attended = outputs[0]
    reduced = lax.psum(jnp.dot(attended, global_down, preferred_element_type=jnp.float32), "row")
    task_scales = select_rows(global_scales, patch_tasks)
    scaled = (reduced * task_scales).astype(jnp.bfloat16)
    mixed = lax.psum_scatter(
        contract(output_weight, attended, 0, 1).astype(jnp.bfloat16),
        "row",
        scatter_dimension=0,
        tiled=True,
    ).astype(jnp.float32)
    mixed = mixed + jnp.transpose(residual.astype(jnp.float32)) + contract(global_up, scaled, 0, 1)
    mixed_b = mixed.astype(jnp.bfloat16)
    own_patches = rows // row_count
    own_bytes = own_patches * PATCH
    rows_in, rows_out = (
        lax.all_gather(hidden_in, "seq", axis=1, tiled=True),
        lax.all_gather(hidden_out, "seq", axis=1, tiled=True),
    )
    partial_value = contract(mixed_b, local_weight, 0, 0)
    projected = lax.psum(partial_value.astype(jnp.bfloat16), "row")
    every = local_inputs(
        byte_ids,
        projected,
        patch_tasks,
        byte_table,
        position_table,
        norm_gain,
        local_down,
        local_scales,
    )
    normed_all = every[2]
    shrunk_all = every[5]
    cotangent_all = lax.all_gather(cotangent, "row", axis=0, tiled=True)
    inputs, inverse, normed, lowered, scales, shrunk, byte_tasks = [
        lax.dynamic_slice_in_dim(value, row_index * own_bytes, own_bytes, 0) for value in every
    ]
    upper = contract(normed_all, rows_in, 1, 1) + jnp.dot(
        shrunk_all, local_up, preferred_element_type=jnp.float32
    )
    through = contract(cotangent_all, rows_out, 1, 1)
    grown = (through * gelu_slope(upper)).astype(jnp.bfloat16)
    grad_local_up = contract(shrunk_all, grown, 0, 0)
    back_norm, back_rank = (
        lax.psum_scatter(
            jnp.dot(grown, rows_in, preferred_element_type=jnp.float32).astype(jnp.bfloat16),
            "row",
            scatter_dimension=0,
            tiled=True,
        ).astype(jnp.float32),
        lax.psum_scatter(
            contract(grown, local_up, 1, 1).astype(jnp.bfloat16),
            "row",
            scatter_dimension=0,
            tiled=True,
        ).astype(jnp.float32),
    )
    grad_local_scales = task_totals(byte_tasks, back_rank * lowered)
    moved = (back_rank * scales).astype(jnp.bfloat16)
    grad_local_down = contract(normed, moved, 0, 0)
    back_total = back_norm + contract(moved, local_down, 1, 1)
    gained = back_total * norm_gain
    average = jnp.mean(gained * inputs, axis=1, keepdims=True)
    back_inputs = cotangent.astype(jnp.float32) + inverse * (
        gained - inputs * inverse * inverse * average
    )
    patch_grad = back_inputs.reshape(own_patches, PATCH, -1).sum(axis=1).astype(jnp.bfloat16)
    back_mixed = contract(
        lax.all_gather(patch_grad, "row", axis=0, tiled=True), local_weight, 1, 1
    ).astype(jnp.bfloat16)
    grad_global_up = contract(scaled, back_mixed, 0, 0)
    back_scaled = lax.psum(contract(back_mixed, global_up, 1, 1), "row")
    grad_global_scales = task_totals(patch_tasks, back_scaled * reduced)
    back_reduced = (back_scaled * task_scales).astype(jnp.bfloat16)
    grad_global_down = contract(attended, back_reduced, 0, 0)
    grad_global_down, grad_global_up, grad_global_scales, grad_local_up = lax.psum(
        (grad_global_down, grad_global_up, grad_global_scales, grad_local_up), "seq"
    )
    grad_local_down, grad_local_scales = lax.psum(
        (grad_local_down, grad_local_scales), ("seq", "row")
    )
    return (
        grad_global_down,
        grad_global_up,
        grad_global_scales,
        grad_local_down,
        grad_local_up,
        grad_local_scales,
    )


MESH = pl.DeviceIdType.MESH
SPAN = 256


def remote(src, dst, send, recv, seq, row):
    return pltpu.make_async_remote_copy(
        src_ref=src,
        dst_ref=dst,
        send_sem=send,
        recv_sem=recv,
        device_id=(seq, row),
        device_id_type=MESH,
    )


def exact(left, right, left_dim, right_dim):
    return lax.dot_general(
        left, right, (((left_dim,), (right_dim,)), ((), ())), precision=lax.Precision.HIGHEST,
        preferred_element_type=jnp.float32,
    )


def split_pair(value):
    high = value.astype(jnp.bfloat16)
    low = (value - high.astype(jnp.float32)).astype(jnp.bfloat16)
    return high, low


def step_kernel(
    chips, depth,
    q_hbm, k_hbm, v_hbm, tasks_hbm, res_hbm, ow_hbm, gd_hbm, gu_hbm, gs_hbm, lw_hbm, ids_hbm,
    table_hbm, pos_hbm, gain_hbm, hi_hbm, ho_hbm, ld_hbm, lu_hbm, ls_hbm, cot_hbm,
    ggd_out, ggu_out, gsc_out, gld_out, glu_out, lsc_out,
    q_ref, k_ref, v_ref, tasks_ref, res_ref, ow_ref, gd_ref, gu_ref, gs_ref, lw_ref, ids_ref,
    pos_ref, gain_ref, ld_ref, ls_ref, cot_ref, wi, wo,
    qb, kb, vb, ob, att, lwb, w2, acc, e1, e1r, mb, mr, bridge,
    emb, inp, nrm, inv, low, sca, bl, gr, mv, bp, bpr, cross, crossr, grads, part, result, full,
    in_sem, a_send, a_recv, f_send, f_recv, o_send, o_recv, z_send, z_recv, x_send, x_recv,
    p_send, p_recv, c_send, c_recv, y_send, y_recv, b_send, b_recv, r_send, r_recv, g_send, g_recv,
):
    bf, f32 = jnp.bfloat16, jnp.float32
    count = 2 * chips
    me = lax.axis_index("seq")
    row = lax.axis_index("row")
    other = 1 - row
    chip, core = me // 2, lax.rem(me, 2)
    mate = 2 * chip + (1 - core)
    rows, width = q_hbm.shape
    half = width // 2
    columns = lw_hbm.shape[1]
    rank = gu_hbm.shape[0]
    wide = columns + HEAD
    shard = hi_hbm.shape[0]
    vocab = table_hbm.shape[0]
    total = rows * PATCH

    def at(number):
        return lax.rem(number + 2 * chips, chips)

    def heads_of(number):
        return pl.ds(pl.multiple_of(number * HEAD, HEAD), HEAD)

    def shard_of(slot):
        return pl.ds(pl.multiple_of(slot * shard, shard), shard)

    barrier = pltpu.get_barrier_semaphore()
    peers = [(lax.rem(me + d, count), row) for d in range(1, count)] + [(me, other)]
    for seq, line in peers:
        pl.semaphore_signal(barrier, inc=1, device_id=(seq, line), device_id_type=MESH)

    loads = {}

    def load(name, src, dst):
        copy = pltpu.make_async_copy(src, dst, in_sem.at[len(loads)])
        copy.start()
        loads[name] = copy

    load("k", k_hbm, k_ref)
    load("v", v_hbm, v_ref)
    load("q", q_hbm, q_ref)
    load("lw", lw_hbm, lw_ref)
    load("hi", hi_hbm, wi.at[shard_of(me)])
    load("ho", ho_hbm, wo.at[shard_of(me)])
    load("cot", cot_hbm, cot_ref.at[row])
    load("gu", gu_hbm, gu_ref)
    load("ow", ow_hbm, ow_ref)
    load("res", res_hbm, res_ref)
    load("gd", gd_hbm, gd_ref.at[pl.ds(0, rank)])
    load("lu", lu_hbm, wi.at[pl.ds(columns, rank)])
    load("ld", ld_hbm, ld_ref.at[pl.ds(0, rank)])
    load("table", table_hbm, emb.at[pl.ds(0, vocab), pl.ds(0, columns)])
    load("tasks", tasks_hbm, tasks_ref)
    load("ids", ids_hbm, ids_ref)
    load("pos", pos_hbm, pos_ref)
    load("gain", gain_hbm, gain_ref)
    load("gs", gs_hbm, gs_ref)
    load("ls", ls_hbm, ls_ref)

    gd_ref[rank:] = jnp.zeros((HEAD - rank, width), bf)
    ld_ref[rank:] = jnp.zeros((HEAD - rank, columns), bf)
    wi[columns + rank :] = jnp.zeros((HEAD - rank, width), bf)
    bridge[...] = jnp.zeros((HEAD, columns), bf)
    emb[:vocab, columns:] = jnp.zeros((vocab, 2 * HEAD), bf)
    emb[vocab + HEAD :] = jnp.zeros((HEAD, wide + HEAD), bf)
    grads[13:] = jnp.zeros((count - 13, 2 * rank, HEAD), bf)

    pl.semaphore_wait(barrier, len(peers))

    own = heads_of(chip)
    arrivals = {}
    forwards = {}
    own_half = pl.ds(pl.multiple_of(core * half, half), half)
    loads["k"].wait()
    loads["v"].wait()
    loads["q"].wait()
    order = sorted(range(1, chips), key=lambda d: -min(d, chips - d))
    for which, (src, dst) in enumerate(
        ((k_ref, kb.at[me]), (v_ref, vb.at[me]), (q_ref, qb.at[chip]))
    ):
        for d in order:
            to = at(chip + d)
            copy = remote(
                src.at[:, heads_of(to)], dst, a_send.at[which, d], a_recv.at[which, d],
                2 * to + core, row,
            )
            copy.start()
            arrivals[which, d] = copy
    for which, (src, dst) in enumerate(((k_ref, kb), (v_ref, vb))):
        copy = remote(
            src.at[:, own], dst.at[me], f_send.at[which, 0], f_recv.at[which, 0], mate, row
        )
        copy.start()
        forwards[which, 0] = copy
    loads["lw"].wait()
    lw_copy = remote(lw_ref.at[own_half], lwb.at[own_half], y_send.at[0], y_recv.at[0], me, other)
    lw_copy.start()
    loads["cot"].wait()
    cot_copy = remote(
        cot_ref.at[row], cot_ref.at[row], c_send.at[0], c_recv.at[0], me, other
    )
    cot_copy.start()

    levels = chips // depth
    level, side = chip // depth, lax.rem(chip, depth)
    loads["hi"].wait()
    loads["ho"].wait()
    weights_in = ((0, wi), (1, wo))
    z_copies = []
    x_copies = []
    p_copies = []
    neighbour = 2 * (level * depth + (1 - side)) + core

    def slot_of(number, line):
        return 2 * (lax.rem(number + levels, levels) * depth + line) + core

    def pass_side(d, slot):
        for which, buffer in weights_in:
            part_of = buffer.at[shard_of(slot)]
            copy = remote(
                part_of, part_of, x_send.at[which, d], x_recv.at[which, d], neighbour, row
            )
            copy.start()
            x_copies.append((d, copy))

    def pass_mate(number, slot):
        for which, buffer in weights_in:
            part_of = buffer.at[shard_of(slot)]
            copy = remote(
                part_of, part_of, p_send.at[which, number], p_recv.at[which, number], mate, row
            )
            copy.start()
            p_copies.append(copy)

    for d in range(1, levels):
        to = lax.rem(level + d, levels) * depth + side
        for which, buffer in weights_in:
            part_of = buffer.at[shard_of(me)]
            copy = remote(
                part_of, part_of, z_send.at[which, d], z_recv.at[which, d], 2 * to + core, row
            )
            copy.start()
            z_copies.append((d, copy))
    pass_side(0, me)
    pass_mate(0, me)

    qb[chip] = q_ref[:, own]
    kb[me] = k_ref[:, own]
    vb[me] = v_ref[:, own]

    loads["gu"].wait()
    mb[...] = jnp.dot(gu_ref[...], lw_ref[...], preferred_element_type=f32).astype(bf)
    m_copy = remote(mb, mr, y_send.at[2], y_recv.at[2], me, other)
    m_copy.start()

    tile = math.gcd(width, SPAN)
    loads["ow"].wait()

    @pl.loop(0, width // tile)
    def _(index):
        block = pl.ds(pl.multiple_of(index * tile, tile), tile)
        acc[block] = jnp.dot(
            ow_ref[block, pl.ds(pl.multiple_of(row * width, width), width)],
            lw_ref[...],
            preferred_element_type=f32,
        )

    lw_copy.wait_recv()
    lw_mate = remote(lwb.at[own_half], lwb.at[own_half], y_send.at[1], y_recv.at[1], mate, row)
    lw_mate.start()
    lw_mate.wait_recv()

    @pl.loop(0, width // tile)
    def _(index):
        block = pl.ds(pl.multiple_of(index * tile, tile), tile)
        summed = acc[block] + jnp.dot(
            ow_ref[block, pl.ds(pl.multiple_of(other * width, width), width)],
            lwb[...],
            preferred_element_type=f32,
        )
        w2[block] = summed.astype(bf)

    for name in ("res", "gd", "lu", "ld", "table", "tasks", "ids", "pos", "gain", "gs", "ls"):
        loads[name].wait()
    picks = (
        lax.broadcasted_iota(jnp.int32, (TASKS, rows), 0) == tasks_ref[...]
    ).astype(f32)

    def widen(table):
        return jnp.concatenate([table, jnp.zeros((TASKS, HEAD - rank), f32)], axis=1)

    task_scales = exact(picks, widen(gs_ref[...]), 0, 0)
    high, low_part = split_pair(exact(picks, widen(ls_ref[...]), 0, 0))
    emb[vocab : vocab + rows, columns:wide] = high
    emb[vocab : vocab + rows, wide:] = low_part
    emb[vocab + rows : vocab + rows + 2 * PATCH, :columns] = jnp.concatenate(
        [pos_ref[...].astype(f32), jnp.zeros((PATCH, columns), f32)], axis=0
    ).astype(bf)
    direct = jnp.dot(res_ref[...], lw_ref[...], preferred_element_type=f32)
    inp[:rows] = direct

    for d in reversed(range(1, chips)):
        for which, buffer in ((0, kb), (1, vb)):
            arrivals[which, d].wait_recv()
            slot = 2 * at(chip - d) + core
            copy = remote(
                buffer.at[slot], buffer.at[slot], f_send.at[which, d], f_recv.at[which, d],
                mate, row,
            )
            copy.start()
            forwards[which, d] = copy
    for d in range(1, chips):
        arrivals[2, d].wait_recv()
    for copy in forwards.values():
        copy.wait_recv()

    factor = 1.0 / math.sqrt(HEAD) / math.log(2.0)
    for i in reversed(range(chips)):
        before = 2 * i * rows
        query = qb[i]
        new_keys = kb[2 * i : 2 * i + 2].reshape(2 * rows, HEAD)
        new_values = vb[2 * i : 2 * i + 2].reshape(2 * rows, HEAD)
        fresh = contract(query, new_keys, 1, 1)
        places = lax.broadcasted_iota(jnp.int32, (rows, 2 * rows), 1)
        queries = lax.broadcasted_iota(jnp.int32, (rows, 2 * rows), 0) + core * rows
        fresh = jnp.where(places <= queries, fresh, -1e30)
        top = jnp.max(fresh, axis=1, keepdims=True)
        if i:
            old_keys = kb[: 2 * i].reshape(before, HEAD)
            old_values = vb[: 2 * i].reshape(before, HEAD)
            scores = contract(query, old_keys, 1, 1)
            top = jnp.maximum(top, jnp.max(scores, axis=1, keepdims=True))
        weights = jnp.exp2((fresh - top) * factor)
        mass = jnp.sum(weights, axis=1, keepdims=True)
        mixed = jnp.dot(weights.astype(bf), new_values, preferred_element_type=f32)
        if i:
            weights = jnp.exp2((scores - top) * factor)
            mass = mass + jnp.sum(weights, axis=1, keepdims=True)
            mixed = mixed + jnp.dot(weights.astype(bf), old_values, preferred_element_type=f32)
        ob[i] = (mixed / mass).astype(bf)

        @pl.when(i != chip)
        def _():
            remote(
                ob.at[i], att.at[:, own], o_send.at[i], o_recv.at[chip], 2 * i + core, row
            ).start()

        @pl.when(i == chip)
        def _():
            att[:, own] = ob[i]

    for d in range(1, levels):
        for number, copy in z_copies:
            if number == d:
                copy.wait_recv()
        slot = slot_of(level - d, side)
        pass_side(d, slot)
        pass_mate(d, slot)
    for d in range(levels):
        for number, copy in x_copies:
            if number == d:
                copy.wait_recv()
        pass_mate(levels + d, slot_of(level - d, 1 - side))

    for i in range(chips):

        @pl.when(i != chip)
        def _():
            back = remote(
                ob.at[i], att.at[:, heads_of(i)], o_send.at[i], o_recv.at[i], 2 * i + core, row
            )
            back.wait_recv()
            back.wait_send()

    attended = att[...]
    e1[:, :columns] = (
        jnp.dot(attended, w2[...], preferred_element_type=f32) + inp[:rows]
    ).astype(bf)
    e1[:, columns:] = contract(attended, gd_ref[...], 1, 1).astype(bf)
    e_copy = remote(e1, e1r, y_send.at[3], y_recv.at[3], me, other)
    e_copy.start()
    cot_copy.wait_recv()
    m_copy.wait_recv()
    bridge[:rank] = (mb[...].astype(f32) + mr[...].astype(f32)).astype(bf)
    belongs = (
        lax.broadcasted_iota(jnp.int32, (rows, total), 1) // PATCH
        == lax.broadcasted_iota(jnp.int32, (rows, total), 0)
    ).astype(f32).astype(bf)
    own_bytes = total // 2
    cot_sum = sum(
        jnp.dot(
            belongs[:, index * own_bytes : (index + 1) * own_bytes], cot_ref[index],
            preferred_element_type=f32,
        )
        for index in range(2)
    )
    e_copy.wait_recv()
    reduced = e1[:, columns:].astype(f32) + e1r[:, columns:].astype(f32)
    scaled = (reduced * task_scales).astype(bf)
    emb[vocab : vocab + rows, :columns] = (
        e1[:, :columns].astype(f32)
        + e1r[:, :columns].astype(f32)
        + jnp.dot(scaled, bridge[...], preferred_element_type=f32)
    ).astype(bf)

    depth_all = emb.shape[0]
    pieces = total // SPAN
    per_piece = SPAN // PATCH

    @pl.loop(0, pieces)
    def _(index):
        block = pl.ds(pl.multiple_of(index * SPAN, SPAN), SPAN)
        line = lax.broadcasted_iota(jnp.int32, (depth_all, SPAN), 0)
        byte = lax.broadcasted_iota(jnp.int32, (depth_all, SPAN), 1) + index * SPAN
        chosen = (
            (line == ids_ref[:, block])
            | (line == vocab + byte // PATCH)
            | (line == vocab + rows + lax.rem(byte, PATCH))
        )
        found = contract(jnp.where(chosen, 1.0, 0.0).astype(bf), emb[...], 0, 0)
        inputs = found[:, :columns]
        scales = found[:, columns:wide] + found[:, wide:]
        inverse = lax.rsqrt(jnp.mean(inputs * inputs, axis=1, keepdims=True) + 1e-06)
        normed = (inputs * inverse * gain_ref[...]).astype(bf)
        lowered = contract(normed, ld_ref[...], 1, 1)
        inp[block] = inputs
        inv[block] = jnp.broadcast_to(inverse, (SPAN, HEAD))
        sca[block] = scales
        low[block] = lowered
        nrm[block, :columns] = normed
        nrm[block, columns:] = (lowered * scales).astype(bf)

    for copy in p_copies:
        copy.wait_recv()

    @pl.loop(0, pieces)
    def _(index):
        block = pl.ds(pl.multiple_of(index * SPAN, SPAN), SPAN)
        upper = jnp.dot(nrm[block], wi[...], preferred_element_type=f32)
        inner = pl.ds(pl.multiple_of(lax.rem(index * SPAN, own_bytes), SPAN), SPAN)
        through = jnp.dot(
            cot_ref[index * SPAN // own_bytes, inner], wo[...], preferred_element_type=f32
        )
        grown = (through * gelu_slope(upper)).astype(bf)
        gr[block] = grown
        both = contract(grown, wi[...], 1, 1)
        back_rank = both[:, columns:]
        moved = (back_rank * sca[block]).astype(bf)
        mv[block] = moved
        bl[block] = back_rank * low[block]
        back_total = both[:, :columns] + jnp.dot(
            moved, ld_ref[...], preferred_element_type=f32
        )
        inputs = inp[block]
        inverse = inv[block][:, :1]
        gained = back_total * gain_ref[...]
        average = jnp.mean(gained * inputs, axis=1, keepdims=True)
        back_inputs = inverse * (gained - inputs * (inverse * inverse * average))
        near = (
            lax.broadcasted_iota(jnp.int32, (per_piece, SPAN), 1) // PATCH
            == lax.broadcasted_iota(jnp.int32, (per_piece, SPAN), 0)
        ).astype(f32).astype(bf)
        patches = pl.ds(pl.multiple_of(index * per_piece, per_piece), per_piece)
        bp[patches] = jnp.dot(
            near, back_inputs.astype(bf), preferred_element_type=f32
        ).astype(bf)
        remote(
            bp.at[patches], bpr.at[patches], b_send.at[index], b_recv.at[index], me, other
        ).start()

    down = contract(mv[...], nrm[:, :columns], 0, 0)[:rank]
    high, low_part = split_pair(bl[...])
    by_patch = jnp.dot(belongs, high, preferred_element_type=f32) + jnp.dot(
        belongs, low_part, preferred_element_type=f32
    )
    small = exact(picks, by_patch, 1, 0)
    small = jnp.concatenate([small, jnp.zeros_like(small)], axis=0)
    cross[:, :columns] = down.astype(bf)
    cross[:, columns:] = small.astype(bf)
    cross_copy = remote(cross, crossr, y_send.at[4], y_recv.at[4], me, other)
    cross_copy.start()
    lift = contract(nrm[:, columns:], gr[...], 0, 0)[:rank].astype(bf)
    spread = width // HEAD
    for t in range(spread):
        grads[t, :rank] = lift[:, t * HEAD : (t + 1) * HEAD]

    for index in range(pieces):
        patches = pl.ds(index * per_piece, per_piece)
        remote(
            bp.at[patches], bpr.at[patches], b_send.at[index], b_recv.at[index], me, other
        ).wait()
    patch_grad = (bp[...].astype(f32) + bpr[...].astype(f32) + cot_sum).astype(bf)
    pulled = contract(scaled, patch_grad, 0, 0)[:rank].astype(bf)
    back_scaled = contract(patch_grad, bridge[...], 1, 1)
    back_reduced = (back_scaled * task_scales).astype(bf)
    outward = contract(back_reduced, att[...], 0, 0)[:rank].astype(bf)
    tops = exact(picks, back_scaled * reduced, 1, 0)
    tops = jnp.concatenate([tops, jnp.zeros_like(tops)], axis=0)
    for t in range(spread):
        grads[t, rank:] = outward[:, t * HEAD : (t + 1) * HEAD]
    cross_copy.wait_recv()
    joint = (cross[...].astype(f32) + crossr[...].astype(f32)).astype(bf)
    thin = columns // HEAD
    for t in range(thin):
        grads[spread + t, :rank] = joint[:, t * HEAD : (t + 1) * HEAD]
        grads[spread + t, rank:] = pulled[:, t * HEAD : (t + 1) * HEAD]
    grads[spread + thin, :rank] = joint[:, columns:]
    grads[spread + thin, rank:] = tops.astype(bf)

    first = []
    for d in range(1, count):
        to = lax.rem(me + d, count)
        copy = remote(grads.at[to], part.at[me], r_send.at[d], r_recv.at[d], to, row)
        copy.start()
        first.append(copy)
    part[me] = grads[me]
    for copy in first:
        copy.wait_recv()
    result[...] = jnp.sum(part[...].astype(f32), axis=0).astype(bf)
    second = []
    for d in range(1, count):
        to = lax.rem(me + d, count)
        copy = remote(result, full.at[me], g_send.at[d], g_recv.at[d], to, row)
        copy.start()
        second.append(copy)
    full[me] = result[...]
    for copy in second:
        copy.wait_recv()
    for t in range(spread):
        glu_out[:, t * HEAD : (t + 1) * HEAD] = full[t, :rank].astype(f32)
        ggd_out[:, t * HEAD : (t + 1) * HEAD] = full[t, rank:].astype(f32)
    for t in range(thin):
        gld_out[:, t * HEAD : (t + 1) * HEAD] = full[spread + t, :rank].astype(f32)
        bridge[:rank, t * HEAD : (t + 1) * HEAD] = full[spread + t, rank:]
    ggu_out[...] = contract(bridge[:rank], lw_ref[...], 1, 1)
    lsc_out[...] = full[spread + thin, :TASKS, :rank].astype(f32)
    gsc_out[...] = full[spread + thin, rank : rank + TASKS, :rank].astype(f32)
    for copy in (
        [lw_copy, lw_mate, cot_copy, m_copy, e_copy, cross_copy]
        + list(arrivals.values())
        + list(forwards.values())
        + [copy for d, copy in z_copies + x_copies]
        + p_copies
        + first
        + second
    ):
        copy.wait_send()


def paired_body(
    patch_queries, patch_keys, patch_values, patch_tasks, residual, output_weight, global_down,
    global_up, global_scales, local_weight, byte_ids, byte_table, position_table, norm_gain,
    hidden_in, hidden_out, local_down, local_up, local_scales, cotangent,
):
    count = lax.axis_size("seq")
    rows, width = patch_queries.shape
    chips = count // 2
    depth = 2
    levels = chips // depth
    columns = local_weight.shape[1]
    rank = global_up.shape[0]
    vocab = byte_table.shape[0]
    total = byte_ids.shape[0]
    wide = columns + HEAD
    pieces = total // SPAN
    bf, f32 = jnp.bfloat16, jnp.float32
    vm = pltpu.VMEM
    dma = pltpu.SemaphoreType.DMA
    args = (
        patch_queries, patch_keys, patch_values, patch_tasks.reshape(1, rows), residual,
        output_weight, jnp.transpose(global_down), global_up, global_scales, local_weight,
        byte_ids.reshape(1, total), byte_table, position_table, norm_gain.reshape(1, columns),
        jnp.transpose(hidden_in), jnp.transpose(hidden_out), jnp.transpose(local_down), local_up,
        local_scales, cotangent,
    )
    outs = pl.pallas_call(
        functools.partial(step_kernel, chips, depth),
        out_shape=(
            jax.ShapeDtypeStruct((rank, width), f32),
            jax.ShapeDtypeStruct((rank, width), f32),
            jax.ShapeDtypeStruct((TASKS, rank), f32),
            jax.ShapeDtypeStruct((rank, columns), f32),
            jax.ShapeDtypeStruct((rank, width), f32),
            jax.ShapeDtypeStruct((TASKS, rank), f32),
        ),
        in_specs=[pl.BlockSpec(memory_space=pl.ANY)] * len(args),
        out_specs=(pl.BlockSpec(memory_space=vm),) * 6,
        scratch_shapes=[
            vm((rows, width), bf), vm((rows, width), bf), vm((rows, width), bf),
            vm((1, rows), jnp.int32), vm((rows, width), bf), vm(output_weight.shape, bf),
            vm((HEAD, width), bf), vm((rank, width), bf), vm((TASKS, rank), f32),
            vm((width, columns), bf), vm((1, total), jnp.int32), vm((PATCH, columns), bf),
            vm((1, columns), f32), vm((HEAD, columns), bf), vm((TASKS, rank), f32),
            vm((2, total // 2, columns), bf), vm((wide, width), bf), vm((columns, width), bf),
            vm((chips, rows, HEAD), bf), vm((count, rows, HEAD), bf), vm((count, rows, HEAD), bf),
            vm((chips, rows, HEAD), bf), vm((rows, width), bf), vm((width, columns), bf),
            vm((width, columns), bf), vm((width, columns), f32), vm((rows, wide), bf),
            vm((rows, wide), bf), vm((rank, columns), bf), vm((rank, columns), bf),
            vm((HEAD, columns), bf),
            vm((vocab + 2 * HEAD, wide + HEAD), bf), vm((total, columns), f32),
            vm((total, wide), bf), vm((total, HEAD), f32), vm((total, HEAD), f32),
            vm((total, HEAD), f32), vm((total, HEAD), f32), vm((total, width), bf),
            vm((total, HEAD), bf), vm((rows, columns), bf), vm((rows, columns), bf),
            vm((rank, wide), bf), vm((rank, wide), bf), vm((count, 2 * rank, HEAD), bf),
            vm((count, 2 * rank, HEAD), bf), vm((2 * rank, HEAD), bf),
            vm((count, 2 * rank, HEAD), bf),
            dma((len(args),)), dma((3, chips)), dma((3, chips)), dma((2, chips)), dma((2, chips)),
            dma((chips,)), dma((chips,)), dma((2, levels)), dma((2, levels)), dma((2, levels)),
            dma((2, levels)), dma((2, chips)), dma((2, chips)), dma((1,)), dma((1,)), dma((5,)),
            dma((5,)), dma((pieces,)), dma((pieces,)), dma((count,)), dma((count,)),
            dma((count,)), dma((count,)),
        ],
        compiler_params=pltpu.CompilerParams(
            collective_id=0, has_side_effects=True, vmem_limit_bytes=60 * 1024 * 1024
        ),
        name="step",
    )(*args)
    ggd, ggu, gsc, gld, glu, lsc = outs
    return (jnp.transpose(ggd), ggu, gsc, jnp.transpose(gld), glu, lsc)


def pick_body(seq_count, row_count, *args):
    heads = args[0].shape[1] // HEAD
    rank = args[7].shape[0]
    hidden = args[14].shape[0]
    fits = (
        row_count == 2
        and seq_count == 2 * heads
        and heads % 4 == 0
        and rank == 2 * TASKS
        and args[0].shape[1] == hidden
        and (4 * rank * hidden) % (seq_count * 16 * HEAD) == 0
        and hidden >= args[9].shape[1] + rank
    )
    return paired_body(*args) if fits else general_body(*args)


def solution(mesh):
    placed = (
        P("seq", "row"),
        P("seq", "row"),
        P("seq", "row"),
        P("seq"),
        P("seq", "row"),
        P("row", None),
        P("row", None),
        P(None, "row"),
        P(),
        P("row", None),
        P("seq"),
        P(),
        P(),
        P(),
        P("row", "seq"),
        P("row", "seq"),
        P(),
        P(None, "row"),
        P(),
        P(("seq", "row"), None),
    )
    chosen = functools.partial(pick_body, mesh.shape["seq"], mesh.shape["row"])
    return jax.shard_map(
        chosen,
        mesh=mesh,
        in_specs=placed,
        out_specs=(P("row", None), P(None, "row"), P(), P(), P(None, "row"), P()),
        check_vma=False,
    )
```

time: 113 us -> 88 us (0.78)
  matrix products: 14.8 us -> 0 us
  other arithmetic: 6.43 us -> 0 us
  Pallas kernels: 83.5 us -> 78.7 us
  local copies, waits for them, and re-layouts: 6.86 us -> 8.33 us
    dot_general x18 -> x0, matrix products: 14.8 us -> none  [the longest x8 4.12 us: contract(): lax.dot_general(left, right, (((left_dim,), (right_dim,)), ((), ())), pre...]
    unnamed x24 -> x6, local copies, waits for them, and re-layouts: 0.95 us -> 8.33 us
    pallas_call x3 -> x1, Pallas kernels: 83.5 us -> 78.7 us  [paired_body(): pl.pallas_call(functools.partial(step_kernel, chips, depth), out_shape=(j...]
    slice x6 -> x0, local copies, waits for them, and re-layouts: 3.52 us -> none  [the longest x2 1.6 us: paired_body(): summed[2 * rank:3 * rank]]
    reduce_sum x2 -> x0, other arithmetic: 3.48 us -> none  [the longest x1 1.92 us: paired_body(): cot_sum = cot.astype(jnp.float32).reshape(patches, PATCH, -1).sum(axis=1)]
    convert_element_type x4 -> x0, other arithmetic: 2.85 us -> none  [the longest x1 0.99 us: paired_body(): patch_grad = (row_sum(back_part) + cot_sum).astype(bf)]
where the time goes in v1:
time: 88 us; the launch traced here: 87.7 us
  Pallas kernels  78.7 us (89%)
  local copies, waits for them, and re-layouts  8.33 us (9%)
    pallas_call x1, Pallas kernels, paired_body(): pl.pallas_call(functools.partial(step_kernel, chips, depth), out_shape=(j...  78.7 us
    unnamed x6, local copies, waits for them, and re-layouts  8.33 us

profile of v1, /device:TPU:0, one launch (start us, length us, event | category | flops | bytes accessed | tf_op | source)
XLA Modules:
  0.0 87.7 jit_solution(6688277288648084209)
XLA Ops:
  0.6 78.7 %step.1 = (f32[16,1024]{1,0:T(8,128)}, f32[16,1024]{1,0:T(8,128)}, f32[8,16]{1,0:T(8,128)}, f32[16,512]{1,0:T(8,128)}, f32[16,1024]{1,0:T(8,128)}, /*index=5*/f32[8,16]{1,0:T(8,128)}) custom-call(bf16[128,1024]{1,0:T(8,128)(2,1)} %q_hbm.1, bf16[128,1024]{1,0:T(8,128)(2,1)} %k_hbm.1, bf16[128,1024]{1,0:T(8,128)(2,1)} %v_hbm.1, s32[1,128]{1,0:T(1,128)} %bitcast.17, ...), custom_call_target="tpu_custom_call" | custom-call | tf_op jit(solution)/shard_map/step/pallas_call | solution.py:777
  79.3 1.5 %copy.32 = f32[1024,16]{0,1:T(8,128)} copy(f32[1024,16]{0,1:T(8,128)} %bitcast.11) | data formatting | bytes 131072
  80.8 1.5 %copy.33 = f32[16,1024]{1,0:T(8,128)} copy(f32[16,1024]{1,0:T(8,128)} %get-tuple-element.25) | data formatting | bytes 131072
  82.3 1.3 %copy.34 = f32[8,16]{1,0:T(8,128)} copy(f32[8,16]{1,0:T(8,128)} %get-tuple-element.26) | data formatting | bytes 1024
  83.5 1.4 %copy.35 = f32[512,16]{0,1:T(8,128)} copy(f32[512,16]{0,1:T(8,128)} %bitcast.13) | data formatting | bytes 65536
  84.9 1.5 %copy.36 = f32[16,1024]{1,0:T(8,128)} copy(f32[16,1024]{1,0:T(8,128)} %get-tuple-element.28) | data formatting | bytes 131072
  86.4 1.3 %copy.37 = f32[8,16]{1,0:T(8,128)} copy(f32[8,16]{1,0:T(8,128)} %get-tuple-element.29) | data formatting | bytes 1024

commit v2 on v1

--- a/solution.py
+++ b/solution.py
@@ -294,14 +294,17 @@
     table_hbm, pos_hbm, gain_hbm, hi_hbm, ho_hbm, ld_hbm, lu_hbm, ls_hbm, cot_hbm,
     ggd_out, ggu_out, gsc_out, gld_out, glu_out, lsc_out,
     q_ref, k_ref, v_ref, tasks_ref, res_ref, ow_ref, gd_ref, gu_ref, gs_ref, lw_ref, ids_ref,
-    pos_ref, gain_ref, ld_ref, ls_ref, cot_ref, wi, wo,
+    pos_ref, gain_ref, ld_ref, ls_ref, cot_ref, wi, wo, wit,
     qb, kb, vb, ob, att, lwb, w2, acc, e1, e1r, mb, mr, bridge,
-    emb, inp, nrm, inv, low, sca, bl, gr, mv, bp, bpr, cross, crossr, grads, part, result, full,
+    red, redr, lif, emb, inp, nrm, inv, low, sca, bl, gr, mv, bp, bpr, cross, crossr,
+    early, early_in, early_full, late, late_in, late_full,
     in_sem, a_send, a_recv, f_send, f_recv, o_send, o_recv, z_send, z_recv, x_send, x_recv,
-    p_send, p_recv, c_send, c_recv, y_send, y_recv, b_send, b_recv, r_send, r_recv, g_send, g_recv,
+    p_send, p_recv, c_send, c_recv, y_send, y_recv, e_send, e_recv, b_send, b_recv,
+    r_send, r_recv, g_send, g_recv,
 ):
     bf, f32 = jnp.bfloat16, jnp.float32
     count = 2 * chips
+    owners = chips
     me = lax.axis_index("seq")
     row = lax.axis_index("row")
     other = 1 - row
@@ -315,9 +318,9 @@
     shard = hi_hbm.shape[0]
     vocab = table_hbm.shape[0]
     total = rows * PATCH
-
-    def at(number):
-        return lax.rem(number + 2 * chips, chips)
+    pieces = total // SPAN
+    per_piece = SPAN // PATCH
+    tiles = width // HEAD + columns // HEAD + 1
 
     def heads_of(number):
         return pl.ds(pl.multiple_of(number * HEAD, HEAD), HEAD)
@@ -337,17 +340,17 @@
         copy.start()
         loads[name] = copy
 
+    load("ho", ho_hbm, wo.at[shard_of(me)])
+    load("hi", hi_hbm, wi.at[shard_of(me)])
     load("k", k_hbm, k_ref)
     load("v", v_hbm, v_ref)
     load("q", q_hbm, q_ref)
     load("lw", lw_hbm, lw_ref)
-    load("hi", hi_hbm, wi.at[shard_of(me)])
-    load("ho", ho_hbm, wo.at[shard_of(me)])
     load("cot", cot_hbm, cot_ref.at[row])
     load("gu", gu_hbm, gu_ref)
     load("ow", ow_hbm, ow_ref)
     load("res", res_hbm, res_ref)
-    load("gd", gd_hbm, gd_ref.at[pl.ds(0, rank)])
+    load("gd", gd_hbm, gd_ref)
     load("lu", lu_hbm, wi.at[pl.ds(columns, rank)])
     load("ld", ld_hbm, ld_ref.at[pl.ds(0, rank)])
     load("table", table_hbm, emb.at[pl.ds(0, vocab), pl.ds(0, columns)])
@@ -358,41 +361,146 @@
     load("gs", gs_hbm, gs_ref)
     load("ls", ls_hbm, ls_ref)
 
-    gd_ref[rank:] = jnp.zeros((HEAD - rank, width), bf)
     ld_ref[rank:] = jnp.zeros((HEAD - rank, columns), bf)
     wi[columns + rank :] = jnp.zeros((HEAD - rank, width), bf)
-    bridge[...] = jnp.zeros((HEAD, columns), bf)
+    emb[vocab : vocab + rows, :columns] = jnp.zeros((rows, columns), bf)
     emb[:vocab, columns:] = jnp.zeros((vocab, 2 * HEAD), bf)
     emb[vocab + HEAD :] = jnp.zeros((HEAD, wide + HEAD), bf)
-    grads[13:] = jnp.zeros((count - 13, 2 * rank, HEAD), bf)
+    for buffer in (early, late):
+        buffer[tiles:] = jnp.zeros((count - tiles, rank, HEAD), bf)
 
     pl.semaphore_wait(barrier, len(peers))
 
     own = heads_of(chip)
-    arrivals = {}
-    forwards = {}
+    near = chips // 2
+    place_in = lax.rem(chip, near)
+    home = chip - place_in
+    away = near - home
     own_half = pl.ds(pl.multiple_of(core * half, half), half)
+
+    def hand(which, to):
+        src, dst = (
+            (k_ref, kb.at[me]), (v_ref, vb.at[me]), (q_ref, qb.at[chip])
+        )[which]
+        return remote(
+            src.at[:, heads_of(to)], dst, a_send.at[which, to], a_recv.at[which, chip],
+            2 * to + core, row,
+        )
+
+    def landed(which, source):
+        dst = (kb.at[2 * source + core], vb.at[2 * source + core], qb.at[source])[which]
+        remote(
+            dst, dst, a_send.at[which, source], a_recv.at[which, source], me, row
+        ).wait_recv()
+
+    targets = [away + lax.rem(place_in + j, near) for j in range(near)] + [
+        home + lax.rem(place_in + j, near) for j in range(1, near)
+    ]
+    levels = chips // depth
+    level, side = chip // depth, lax.rem(chip, depth)
+    weights_in = ((1, wo), (0, wi))
+    neighbour = 2 * (level * depth + (1 - side)) + core
+
+    def slot_of(number, line):
+        return 2 * (number * depth + line) + core
+
+    def move(which, slot, sends, recvs, to):
+        buffer = wo if which else wi
+        piece = buffer.at[shard_of(slot)]
+        return remote(piece, piece, sends, recvs, to, row)
+
+    def pass_along(which, source):
+        slot = slot_of(source, side)
+        for way, step in ((0, 1), (1, -1)):
+            ahead = level + step
+            fits = (ahead >= 0) & (ahead < levels) & ((source - level) * step <= 0)
+
+            @pl.when(fits)
+            def _():
+                move(
+                    which, slot, z_send.at[which, source, way], z_recv.at[which, source],
+                    slot_of(ahead, side),
+                ).start()
+
+    def settle_along(which, source):
+        slot = slot_of(source, side)
+        for way, step in ((0, 1), (1, -1)):
+            ahead = level + step
+            fits = (ahead >= 0) & (ahead < levels) & ((source - level) * step <= 0)
+
+            @pl.when(fits)
+            def _():
+                move(
+                    which, slot, z_send.at[which, source, way], z_recv.at[which, source],
+                    slot_of(ahead, side),
+                ).wait_send()
+
+    def across(which, source, line):
+        return move(
+            which, slot_of(source, line), x_send.at[which, source], x_recv.at[which, source],
+            neighbour,
+        )
+
+    def to_mate(which, source, line):
+        number = jnp.where(line == side, source, levels + source)
+        return move(
+            which, slot_of(source, line), p_send.at[which, number], p_recv.at[which, number], mate
+        )
+
+    def relay(hop):
+        for which, buffer in weights_in:
+            for source in (level - hop, level + hop):
+
+                @pl.when((source >= 0) & (source < levels))
+                def _():
+                    move(
+                        which, slot_of(source, side), z_send.at[which, source, 0],
+                        z_recv.at[which, source], me,
+                    ).wait_recv()
+                    pass_along(which, source)
+                    across(which, source, side).start()
+                    to_mate(which, source, side).start()
+
+    def cross_over(hop):
+        for which, buffer in weights_in:
+            for source in {0: (level,)}.get(hop, (level - hop, level + hop)):
+
+                @pl.when((source >= 0) & (source < levels))
+                def _():
+                    across(which, source, 1 - side).wait_recv()
+                    to_mate(which, source, 1 - side).start()
+
+    loads["ho"].wait()
+    loads["hi"].wait()
+    for which, buffer in weights_in:
+        pass_along(which, level)
+        across(which, level, side).start()
+        to_mate(which, level, side).start()
+
     loads["k"].wait()
     loads["v"].wait()
     loads["q"].wait()
-    order = sorted(range(1, chips), key=lambda d: -min(d, chips - d))
-    for which, (src, dst) in enumerate(
-        ((k_ref, kb.at[me]), (v_ref, vb.at[me]), (q_ref, qb.at[chip]))
-    ):
-        for d in order:
-            to = at(chip + d)
-            copy = remote(
-                src.at[:, heads_of(to)], dst, a_send.at[which, d], a_recv.at[which, d],
-                2 * to + core, row,
-            )
-            copy.start()
-            arrivals[which, d] = copy
-    for which, (src, dst) in enumerate(((k_ref, kb), (v_ref, vb))):
-        copy = remote(
-            src.at[:, own], dst.at[me], f_send.at[which, 0], f_recv.at[which, 0], mate, row
-        )
-        copy.start()
-        forwards[which, 0] = copy
+
+
+    def share(which, source):
+        buffer = (kb, vb)[which]
+        slot = 2 * source + core
+        return remote(
+            buffer.at[slot], buffer.at[slot], f_send.at[which, source], f_recv.at[which, source],
+            mate, row,
+        )
+
+    kb[me] = k_ref[:, own]
+    vb[me] = v_ref[:, own]
+    qb[chip] = q_ref[:, own]
+    for to in targets:
+        for which in range(2):
+            hand(which, to).start()
+    for which, src in enumerate((k_ref, v_ref)):
+        remote(
+            src.at[:, own], (kb, vb)[which].at[me], f_send.at[which, chip],
+            f_recv.at[which, chip], mate, row,
+        ).start()
     loads["lw"].wait()
     lw_copy = remote(lw_ref.at[own_half], lwb.at[own_half], y_send.at[0], y_recv.at[0], me, other)
     lw_copy.start()
@@ -401,53 +509,6 @@
         cot_ref.at[row], cot_ref.at[row], c_send.at[0], c_recv.at[0], me, other
     )
     cot_copy.start()
-
-    levels = chips // depth
-    level, side = chip // depth, lax.rem(chip, depth)
-    loads["hi"].wait()
-    loads["ho"].wait()
-    weights_in = ((0, wi), (1, wo))
-    z_copies = []
-    x_copies = []
-    p_copies = []
-    neighbour = 2 * (level * depth + (1 - side)) + core
-
-    def slot_of(number, line):
-        return 2 * (lax.rem(number + levels, levels) * depth + line) + core
-
-    def pass_side(d, slot):
-        for which, buffer in weights_in:
-            part_of = buffer.at[shard_of(slot)]
-            copy = remote(
-                part_of, part_of, x_send.at[which, d], x_recv.at[which, d], neighbour, row
-            )
-            copy.start()
-            x_copies.append((d, copy))
-
-    def pass_mate(number, slot):
-        for which, buffer in weights_in:
-            part_of = buffer.at[shard_of(slot)]
-            copy = remote(
-                part_of, part_of, p_send.at[which, number], p_recv.at[which, number], mate, row
-            )
-            copy.start()
-            p_copies.append(copy)
-
-    for d in range(1, levels):
-        to = lax.rem(level + d, levels) * depth + side
-        for which, buffer in weights_in:
-            part_of = buffer.at[shard_of(me)]
-            copy = remote(
-                part_of, part_of, z_send.at[which, d], z_recv.at[which, d], 2 * to + core, row
-            )
-            copy.start()
-            z_copies.append((d, copy))
-    pass_side(0, me)
-    pass_mate(0, me)
-
-    qb[chip] = q_ref[:, own]
-    kb[me] = k_ref[:, own]
-    vb[me] = v_ref[:, own]
 
     loads["gu"].wait()
     mb[...] = jnp.dot(gu_ref[...], lw_ref[...], preferred_element_type=f32).astype(bf)
@@ -466,11 +527,94 @@
             preferred_element_type=f32,
         )
 
+    relay(1)
+    for to in targets:
+        hand(2, to).start()
+    cross_over(0)
+    for j in range(1, near):
+        source = home + lax.rem(place_in + near - j, near)
+        for which in range(2):
+            landed(which, source)
+            share(which, source).start()
+    for j in range(near):
+        source = away + lax.rem(place_in + near - j, near)
+        for which in range(2):
+            landed(which, source)
+            share(which, source).start()
+    for source in range(chips):
+        for which in range(2):
+            buffer = (kb, vb)[which]
+            slot = 2 * source + 1 - core
+            remote(
+                buffer.at[slot], buffer.at[slot], f_send.at[which, source],
+                f_recv.at[which, source], mate, row,
+            ).wait_recv()
+
     lw_copy.wait_recv()
     lw_mate = remote(lwb.at[own_half], lwb.at[own_half], y_send.at[1], y_recv.at[1], mate, row)
     lw_mate.start()
+    factor = 1.0 / math.sqrt(HEAD) / math.log(2.0)
+    span = chips * rows
+
+    def attend(i, late_half):
+        query = qb[i]
+        start = chips if late_half else 0
+        fresh = contract(query, kb[start : start + chips].reshape(span, HEAD), 1, 1)
+        places = lax.broadcasted_iota(jnp.int32, (rows, span), 1)
+        queries = lax.broadcasted_iota(jnp.int32, (rows, span), 0) + (
+            (2 * i + core - start) * rows
+        )
+        fresh = jnp.where(places <= queries, fresh, -1e30)
+        top = jnp.max(fresh, axis=1, keepdims=True)
+        if late_half:
+            scores = contract(query, kb[:start].reshape(span, HEAD), 1, 1)
+            top = jnp.maximum(top, jnp.max(scores, axis=1, keepdims=True))
+        weights = jnp.exp2((fresh - top) * factor)
+        mass = jnp.sum(weights, axis=1, keepdims=True)
+        mixed = jnp.dot(
+            weights.astype(bf), vb[start : start + chips].reshape(span, HEAD),
+            preferred_element_type=f32,
+        )
+        if late_half:
+            weights = jnp.exp2((scores - top) * factor)
+            mass = mass + jnp.sum(weights, axis=1, keepdims=True)
+            mixed = mixed + jnp.dot(
+                weights.astype(bf), vb[:start].reshape(span, HEAD), preferred_element_type=f32
+            )
+        ob[i] = (mixed / mass).astype(bf)
+
+    @pl.loop(0, chips)
+    def _(step):
+        @pl.when(step == 1)
+        def _():
+            relay(2)
+            cross_over(1)
+
+        at_home = (step < near - 1) | (step == chips - 1)
+        stage = jnp.where(at_home, lax.rem(step + 1, near), step - (near - 1))
+        i = jnp.where(at_home, home, away) + lax.rem(place_in + near - stage, near)
+
+        @pl.when(i != chip)
+        def _():
+            landed(2, i)
+
+        @pl.when(i < near)
+        def _():
+            attend(i, False)
+
+        @pl.when(i >= near)
+        def _():
+            attend(i, True)
+
+        @pl.when(i != chip)
+        def _():
+            remote(
+                ob.at[i], att.at[:, own], o_send.at[i], o_recv.at[chip], 2 * i + core, row
+            ).start()
+
+    att[:, own] = ob[chip]
+
     lw_mate.wait_recv()
-
     @pl.loop(0, width // tile)
     def _(index):
         block = pl.ds(pl.multiple_of(index * tile, tile), tile)
@@ -490,7 +634,7 @@
     def widen(table):
         return jnp.concatenate([table, jnp.zeros((TASKS, HEAD - rank), f32)], axis=1)
 
-    task_scales = exact(picks, widen(gs_ref[...]), 0, 0)
+    task_scales = exact(gs_ref[...], picks, 0, 0)
     high, low_part = split_pair(exact(picks, widen(ls_ref[...]), 0, 0))
     emb[vocab : vocab + rows, columns:wide] = high
     emb[vocab : vocab + rows, wide:] = low_part
@@ -500,89 +644,9 @@
     direct = jnp.dot(res_ref[...], lw_ref[...], preferred_element_type=f32)
     inp[:rows] = direct
 
-    for d in reversed(range(1, chips)):
-        for which, buffer in ((0, kb), (1, vb)):
-            arrivals[which, d].wait_recv()
-            slot = 2 * at(chip - d) + core
-            copy = remote(
-                buffer.at[slot], buffer.at[slot], f_send.at[which, d], f_recv.at[which, d],
-                mate, row,
-            )
-            copy.start()
-            forwards[which, d] = copy
-    for d in range(1, chips):
-        arrivals[2, d].wait_recv()
-    for copy in forwards.values():
-        copy.wait_recv()
-
-    factor = 1.0 / math.sqrt(HEAD) / math.log(2.0)
-    for i in reversed(range(chips)):
-        before = 2 * i * rows
-        query = qb[i]
-        new_keys = kb[2 * i : 2 * i + 2].reshape(2 * rows, HEAD)
-        new_values = vb[2 * i : 2 * i + 2].reshape(2 * rows, HEAD)
-        fresh = contract(query, new_keys, 1, 1)
-        places = lax.broadcasted_iota(jnp.int32, (rows, 2 * rows), 1)
-        queries = lax.broadcasted_iota(jnp.int32, (rows, 2 * rows), 0) + core * rows
-        fresh = jnp.where(places <= queries, fresh, -1e30)
-        top = jnp.max(fresh, axis=1, keepdims=True)
-        if i:
-            old_keys = kb[: 2 * i].reshape(before, HEAD)
-            old_values = vb[: 2 * i].reshape(before, HEAD)
-            scores = contract(query, old_keys, 1, 1)
-            top = jnp.maximum(top, jnp.max(scores, axis=1, keepdims=True))
-        weights = jnp.exp2((fresh - top) * factor)
-        mass = jnp.sum(weights, axis=1, keepdims=True)
-        mixed = jnp.dot(weights.astype(bf), new_values, preferred_element_type=f32)
-        if i:
-            weights = jnp.exp2((scores - top) * factor)
-            mass = mass + jnp.sum(weights, axis=1, keepdims=True)
-            mixed = mixed + jnp.dot(weights.astype(bf), old_values, preferred_element_type=f32)
-        ob[i] = (mixed / mass).astype(bf)
-
-        @pl.when(i != chip)
-        def _():
-            remote(
-                ob.at[i], att.at[:, own], o_send.at[i], o_recv.at[chip], 2 * i + core, row
-            ).start()
-
-        @pl.when(i == chip)
-        def _():
-            att[:, own] = ob[i]
-
-    for d in range(1, levels):
-        for number, copy in z_copies:
-            if number == d:
-                copy.wait_recv()
-        slot = slot_of(level - d, side)
-        pass_side(d, slot)
-        pass_mate(d, slot)
-    for d in range(levels):
-        for number, copy in x_copies:
-            if number == d:
-                copy.wait_recv()
-        pass_mate(levels + d, slot_of(level - d, 1 - side))
-
-    for i in range(chips):
-
-        @pl.when(i != chip)
-        def _():
-            back = remote(
-                ob.at[i], att.at[:, heads_of(i)], o_send.at[i], o_recv.at[i], 2 * i + core, row
-            )
-            back.wait_recv()
-            back.wait_send()
-
-    attended = att[...]
-    e1[:, :columns] = (
-        jnp.dot(attended, w2[...], preferred_element_type=f32) + inp[:rows]
-    ).astype(bf)
-    e1[:, columns:] = contract(attended, gd_ref[...], 1, 1).astype(bf)
-    e_copy = remote(e1, e1r, y_send.at[3], y_recv.at[3], me, other)
-    e_copy.start()
     cot_copy.wait_recv()
     m_copy.wait_recv()
-    bridge[:rank] = (mb[...].astype(f32) + mr[...].astype(f32)).astype(bf)
+    bridge[...] = (mb[...].astype(f32) + mr[...].astype(f32)).astype(bf)
     belongs = (
         lax.broadcasted_iota(jnp.int32, (rows, total), 1) // PATCH
         == lax.broadcasted_iota(jnp.int32, (rows, total), 0)
@@ -595,22 +659,56 @@
         )
         for index in range(2)
     )
-    e_copy.wait_recv()
-    reduced = e1[:, columns:].astype(f32) + e1r[:, columns:].astype(f32)
+
+    for hop in range(3, levels):
+        relay(hop)
+    for hop in range(2, levels - 1):
+        cross_over(hop)
+    for i in range(chips):
+
+        @pl.when(i != chip)
+        def _():
+            back = remote(
+                ob.at[i], att.at[:, heads_of(i)], o_send.at[i], o_recv.at[i], 2 * i + core, row
+            )
+            back.wait_recv()
+            back.wait_send()
+
+    e_copies = []
+    red[...] = contract(gd_ref[...], att[...], 1, 1).astype(bf)
+    red_copy = remote(red, redr, y_send.at[3], y_recv.at[3], me, other)
+    red_copy.start()
+    e1[...] = (
+        jnp.dot(att[...], w2[...], preferred_element_type=f32) + inp[:rows]
+    ).astype(bf)
+    for index in range(pieces):
+        patches = pl.ds(index * per_piece, per_piece)
+        copy = remote(e1.at[patches], e1r.at[patches], e_send.at[index], e_recv.at[index], me, other)
+        copy.start()
+        e_copies.append(copy)
+    red_copy.wait_recv()
+    reduced = red[...].astype(f32) + redr[...].astype(f32)
     scaled = (reduced * task_scales).astype(bf)
-    emb[vocab : vocab + rows, :columns] = (
-        e1[:, :columns].astype(f32)
-        + e1r[:, :columns].astype(f32)
-        + jnp.dot(scaled, bridge[...], preferred_element_type=f32)
-    ).astype(bf)
+    lifted = contract(scaled, bridge[...], 0, 0)
 
     depth_all = emb.shape[0]
-    pieces = total // SPAN
-    per_piece = SPAN // PATCH
+    lif[...] = lifted
 
     @pl.loop(0, pieces)
     def _(index):
         block = pl.ds(pl.multiple_of(index * SPAN, SPAN), SPAN)
+        patches = pl.ds(pl.multiple_of(index * per_piece, per_piece), per_piece)
+        remote(
+            e1.at[patches], e1r.at[patches], e_send.at[index], e_recv.at[index], me, other
+        ).wait_recv()
+        emb[pl.ds(pl.multiple_of(vocab + index * per_piece, per_piece), per_piece), :columns] = (
+            e1[patches].astype(f32) + e1r[patches].astype(f32) + lif[patches]
+        ).astype(bf)
+
+        @pl.when(index == pieces // 2)
+        def _():
+            cross_over(levels - 1)
+
         line = lax.broadcasted_iota(jnp.int32, (depth_all, SPAN), 0)
         byte = lax.broadcasted_iota(jnp.int32, (depth_all, SPAN), 1) + index * SPAN
         chosen = (
@@ -631,9 +729,14 @@
         nrm[block, :columns] = normed
         nrm[block, columns:] = (lowered * scales).astype(bf)
 
-    for copy in p_copies:
-        copy.wait_recv()
-
+    def mates_weights(which):
+        for source in range(levels):
+            for line in (side, 1 - side):
+                to_mate(which, source, line).wait_recv()
+
+    mates_weights(1)
+    mates_weights(0)
+    wit[...] = jnp.transpose(wi[...])
     @pl.loop(0, pieces)
     def _(index):
         block = pl.ds(pl.multiple_of(index * SPAN, SPAN), SPAN)
@@ -644,7 +747,7 @@
         )
         grown = (through * gelu_slope(upper)).astype(bf)
         gr[block] = grown
-        both = contract(grown, wi[...], 1, 1)
+        both = jnp.dot(grown, wit[...], preferred_element_type=f32)
         back_rank = both[:, columns:]
         moved = (back_rank * sca[block]).astype(bf)
         mv[block] = moved
@@ -682,8 +785,77 @@
     cross_copy.start()
     lift = contract(nrm[:, columns:], gr[...], 0, 0)[:rank].astype(bf)
     spread = width // HEAD
+    thin = columns // HEAD
     for t in range(spread):
-        grads[t, :rank] = lift[:, t * HEAD : (t + 1) * HEAD]
+        early[t] = lift[:, t * HEAD : (t + 1) * HEAD]
+    base = owners // 2
+
+    def spread_out(kind, source, landing, first, last):
+        for t in range(first, last):
+            to = base + t
+
+            @pl.when(to != me)
+            def _():
+                remote(
+                    source.at[pl.ds(2 * t, 2)], landing.at[me], r_send.at[kind, t],
+                    r_recv.at[kind, me], to, row,
+                ).start()
+
+            @pl.when(to == me)
+            def _():
+                landing[me] = source[2 * t : 2 * t + 2]
+
+    def settle_out(kind, source, landing):
+        for t in range(owners):
+            to = base + t
+
+            @pl.when(to != me)
+            def _():
+                remote(
+                    source.at[pl.ds(2 * t, 2)], landing.at[me], r_send.at[kind, t],
+                    r_recv.at[kind, me], to, row,
+                ).wait_send()
+
+    mine = (me >= base) & (me < base + owners)
+    place = jnp.where(mine, me - base, 0)
+
+    def gather_in(kind, landing, final):
+        @pl.when(mine)
+        def _():
+            for d in range(1, count):
+                source = lax.rem(me + d, count)
+                remote(
+                    landing.at[source], landing.at[source], r_send.at[kind, 0],
+                    r_recv.at[kind, source], me, row,
+                ).wait_recv()
+            final[place] = jnp.sum(landing[...].astype(f32), axis=0).astype(bf)
+            for d in range(1, count):
+                to = lax.rem(me + d, count)
+                remote(
+                    final.at[place], final.at[place], g_send.at[kind, d],
+                    g_recv.at[kind, place], to, row,
+                ).start()
+
+    def finish_in(kind, final):
+        for t in range(owners):
+
+            @pl.when(me != base + t)
+            def _():
+                remote(
+                    final.at[t], final.at[t], g_send.at[kind, 0], g_recv.at[kind, t], me, row
+                ).wait_recv()
+
+    def settle_in(kind, final):
+        @pl.when(mine)
+        def _():
+            for d in range(1, count):
+                to = lax.rem(me + d, count)
+                remote(
+                    final.at[place], final.at[place], g_send.at[kind, d],
+                    g_recv.at[kind, place], to, row,
+                ).wait_send()
+
+    spread_out(0, early, early_in, 0, spread // 2)
 
     for index in range(pieces):
         patches = pl.ds(index * per_piece, per_piece)
@@ -691,61 +863,70 @@
             bp.at[patches], bpr.at[patches], b_send.at[index], b_recv.at[index], me, other
         ).wait()
     patch_grad = (bp[...].astype(f32) + bpr[...].astype(f32) + cot_sum).astype(bf)
-    pulled = contract(scaled, patch_grad, 0, 0)[:rank].astype(bf)
-    back_scaled = contract(patch_grad, bridge[...], 1, 1)
+    pulled = jnp.dot(scaled, patch_grad, preferred_element_type=f32).astype(bf)
+    back_scaled = contract(bridge[...], patch_grad, 1, 1)
     back_reduced = (back_scaled * task_scales).astype(bf)
-    outward = contract(back_reduced, att[...], 0, 0)[:rank].astype(bf)
-    tops = exact(picks, back_scaled * reduced, 1, 0)
+    outward = jnp.dot(back_reduced, att[...], preferred_element_type=f32).astype(bf)
+    product = back_scaled * reduced
+    product = jnp.concatenate([product, jnp.zeros((HEAD - rank, rows), f32)], axis=0)
+    tops = exact(picks, product, 1, 1)
     tops = jnp.concatenate([tops, jnp.zeros_like(tops)], axis=0)
     for t in range(spread):
-        grads[t, rank:] = outward[:, t * HEAD : (t + 1) * HEAD]
+        late[t] = outward[:, t * HEAD : (t + 1) * HEAD]
+    for t in range(thin):
+        late[spread + t] = pulled[:, t * HEAD : (t + 1) * HEAD]
+    late[spread + thin] = tops.astype(bf)
+    spread_out(1, late, late_in, 0, owners)
     cross_copy.wait_recv()
     joint = (cross[...].astype(f32) + crossr[...].astype(f32)).astype(bf)
-    thin = columns // HEAD
     for t in range(thin):
-        grads[spread + t, :rank] = joint[:, t * HEAD : (t + 1) * HEAD]
-        grads[spread + t, rank:] = pulled[:, t * HEAD : (t + 1) * HEAD]
-    grads[spread + thin, :rank] = joint[:, columns:]
-    grads[spread + thin, rank:] = tops.astype(bf)
-
-    first = []
-    for d in range(1, count):
-        to = lax.rem(me + d, count)
-        copy = remote(grads.at[to], part.at[me], r_send.at[d], r_recv.at[d], to, row)
-        copy.start()
-        first.append(copy)
-    part[me] = grads[me]
-    for copy in first:
-        copy.wait_recv()
-    result[...] = jnp.sum(part[...].astype(f32), axis=0).astype(bf)
-    second = []
-    for d in range(1, count):
-        to = lax.rem(me + d, count)
-        copy = remote(result, full.at[me], g_send.at[d], g_recv.at[d], to, row)
-        copy.start()
-        second.append(copy)
-    full[me] = result[...]
-    for copy in second:
-        copy.wait_recv()
+        early[spread + t] = joint[:, t * HEAD : (t + 1) * HEAD]
+    early[spread + thin] = joint[:, columns:]
+    spread_out(0, early, early_in, spread // 2, owners)
+    gather_in(0, early_in, early_full)
+    gather_in(1, late_in, late_full)
+    finish_in(0, early_full)
+
+    def tile_of(final, t):
+        return final[t // 2, t % 2]
+
     for t in range(spread):
-        glu_out[:, t * HEAD : (t + 1) * HEAD] = full[t, :rank].astype(f32)
-        ggd_out[:, t * HEAD : (t + 1) * HEAD] = full[t, rank:].astype(f32)
+        glu_out[:, t * HEAD : (t + 1) * HEAD] = tile_of(early_full, t).astype(f32)
     for t in range(thin):
-        gld_out[:, t * HEAD : (t + 1) * HEAD] = full[spread + t, :rank].astype(f32)
-        bridge[:rank, t * HEAD : (t + 1) * HEAD] = full[spread + t, rank:]
-    ggu_out[...] = contract(bridge[:rank], lw_ref[...], 1, 1)
-    lsc_out[...] = full[spread + thin, :TASKS, :rank].astype(f32)
-    gsc_out[...] = full[spread + thin, rank : rank + TASKS, :rank].astype(f32)
-    for copy in (
-        [lw_copy, lw_mate, cot_copy, m_copy, e_copy, cross_copy]
-        + list(arrivals.values())
-        + list(forwards.values())
-        + [copy for d, copy in z_copies + x_copies]
-        + p_copies
-        + first
-        + second
+        gld_out[:, t * HEAD : (t + 1) * HEAD] = tile_of(early_full, spread + t).astype(f32)
+    lsc_out[...] = tile_of(early_full, spread + thin)[:TASKS, :rank].astype(f32)
+    finish_in(1, late_full)
+    for t in range(spread):
+        ggd_out[:, t * HEAD : (t + 1) * HEAD] = tile_of(late_full, t).astype(f32)
+    for t in range(thin):
+        bridge[:, t * HEAD : (t + 1) * HEAD] = tile_of(late_full, spread + t)
+    ggu_out[...] = contract(bridge[...], lw_ref[...], 1, 1)
+    gsc_out[...] = tile_of(late_full, spread + thin)[:TASKS, :rank].astype(f32)
+    for kind, source, landing, final in (
+        (0, early, early_in, early_full), (1, late, late_in, late_full)
     ):
+        settle_out(kind, source, landing)
+        settle_in(kind, final)
+    for which, buffer in weights_in:
+        for source in range(levels):
+            settle_along(which, source)
+            across(which, source, side).wait_send()
+            for line in (side, 1 - side):
+                to_mate(which, source, line).wait_send()
+    for to in targets:
+        for which in range(3):
+            hand(which, to).wait_send()
+    for source in range(chips):
+        for which in range(2):
+            share(which, source).wait_send()
+    for copy in [lw_copy, lw_mate, cot_copy, m_copy, red_copy, cross_copy] + e_copies:
         copy.wait_send()
+
+
+def copy_kernel(*refs):
+    number = len(refs) // 2
+    for source, target in zip(refs[:number], refs[number:]):
+        target[...] = source[...]
 
 
 def paired_body(
@@ -789,34 +970,47 @@
         scratch_shapes=[
             vm((rows, width), bf), vm((rows, width), bf), vm((rows, width), bf),
             vm((1, rows), jnp.int32), vm((rows, width), bf), vm(output_weight.shape, bf),
-            vm((HEAD, width), bf), vm((rank, width), bf), vm((TASKS, rank), f32),
+            vm((rank, width), bf), vm((rank, width), bf), vm((TASKS, rank), f32),
             vm((width, columns), bf), vm((1, total), jnp.int32), vm((PATCH, columns), bf),
             vm((1, columns), f32), vm((HEAD, columns), bf), vm((TASKS, rank), f32),
             vm((2, total // 2, columns), bf), vm((wide, width), bf), vm((columns, width), bf),
+            vm((width, wide), bf),
             vm((chips, rows, HEAD), bf), vm((count, rows, HEAD), bf), vm((count, rows, HEAD), bf),
             vm((chips, rows, HEAD), bf), vm((rows, width), bf), vm((width, columns), bf),
-            vm((width, columns), bf), vm((width, columns), f32), vm((rows, wide), bf),
-            vm((rows, wide), bf), vm((rank, columns), bf), vm((rank, columns), bf),
-            vm((HEAD, columns), bf),
+            vm((width, columns), bf), vm((width, columns), f32), vm((rows, columns), bf),
+            vm((rows, columns), bf), vm((rank, columns), bf), vm((rank, columns), bf),
+            vm((rank, columns), bf), vm((rank, rows), bf), vm((rank, rows), bf),
+            vm((rows, columns), f32),
             vm((vocab + 2 * HEAD, wide + HEAD), bf), vm((total, columns), f32),
             vm((total, wide), bf), vm((total, HEAD), f32), vm((total, HEAD), f32),
             vm((total, HEAD), f32), vm((total, HEAD), f32), vm((total, width), bf),
             vm((total, HEAD), bf), vm((rows, columns), bf), vm((rows, columns), bf),
-            vm((rank, wide), bf), vm((rank, wide), bf), vm((count, 2 * rank, HEAD), bf),
-            vm((count, 2 * rank, HEAD), bf), vm((2 * rank, HEAD), bf),
-            vm((count, 2 * rank, HEAD), bf),
+            vm((rank, wide), bf), vm((rank, wide), bf),
+        ]
+        + [
+            vm((count, rank, HEAD), bf), vm((count, 2, rank, HEAD), bf),
+            vm((chips, 2, rank, HEAD), bf),
+        ]
+        * 2
+        + [
             dma((len(args),)), dma((3, chips)), dma((3, chips)), dma((2, chips)), dma((2, chips)),
-            dma((chips,)), dma((chips,)), dma((2, levels)), dma((2, levels)), dma((2, levels)),
+            dma((chips,)), dma((chips,)), dma((2, levels, 2)), dma((2, levels)), dma((2, levels)),
             dma((2, levels)), dma((2, chips)), dma((2, chips)), dma((1,)), dma((1,)), dma((5,)),
-            dma((5,)), dma((pieces,)), dma((pieces,)), dma((count,)), dma((count,)),
-            dma((count,)), dma((count,)),
+            dma((5,)), dma((pieces,)), dma((pieces,)), dma((pieces,)), dma((pieces,)),
+            dma((2, chips)), dma((2, count)), dma((2, count)), dma((2, chips)),
         ],
         compiler_params=pltpu.CompilerParams(
             collective_id=0, has_side_effects=True, vmem_limit_bytes=60 * 1024 * 1024
         ),
         name="step",
     )(*args)
-    ggd, ggu, gsc, gld, glu, lsc = outs
+    ggd, ggu, gsc, gld, glu, lsc = pl.pallas_call(
+        copy_kernel,
+        out_shape=tuple(jax.ShapeDtypeStruct(item.shape, item.dtype) for item in outs),
+        in_specs=[pl.BlockSpec(memory_space=vm)] * len(outs),
+        out_specs=(pl.BlockSpec(memory_space=vm),) * len(outs),
+        name="spill",
+    )(*outs)
     return (jnp.transpose(ggd), ggu, gsc, jnp.transpose(gld), glu, lsc)
 
 
@@ -831,7 +1025,8 @@
         and rank == 2 * TASKS
         and args[0].shape[1] == hidden
         and (4 * rank * hidden) % (seq_count * 16 * HEAD) == 0
-        and hidden >= args[9].shape[1] + rank
+        and hidden // HEAD + args[9].shape[1] // HEAD < seq_count
+        and args[0].shape[0] == HEAD
     )
     return paired_body(*args) if fits else general_body(*args)
 

time: 88 us -> 70.4 us (0.80)
  Pallas kernels: 78.7 us -> 69.6 us
  local copies, waits for them, and re-layouts: 8.33 us -> 0 us
    pallas_call x1, Pallas kernels: 78.7 us -> 67.9 us  [paired_body(): pl.pallas_call(functools.partial(step_kernel, chips, depth), out_shape=(j...]
    unnamed x6 -> x0, local copies, waits for them, and re-layouts: 8.33 us -> none
    pallas_call x0 -> x1, Pallas kernels: none -> 1.63 us  [paired_body(): pl.pallas_call(copy_kernel, out_shape=tuple((jax.ShapeDtypeStruct(item.sh...]
where the time goes in v2:
time: 70.4 us; the launch traced here: 70.2 us
  Pallas kernels  69.6 us (99%)
    pallas_call x1, Pallas kernels, paired_body(): pl.pallas_call(functools.partial(step_kernel, chips, depth), out_shape=(j...  67.9 us
    pallas_call x1, Pallas kernels, paired_body(): pl.pallas_call(copy_kernel, out_shape=tuple((jax.ShapeDtypeStruct(item.sh...  1.63 us

profile of v2, /device:TPU:0, one launch (start us, length us, event | category | flops | bytes accessed | tf_op | source)
XLA Modules:
  0.0 70.2 jit_solution(9212605474529082364)
XLA Ops:
  0.6 67.9 %step.1 = (f32[16,1024]{1,0:T(8,128)}, f32[16,1024]{1,0:T(8,128)}, f32[8,16]{1,0:T(8,128)}, f32[16,512]{1,0:T(8,128)}, f32[16,1024]{1,0:T(8,128)}, /*index=5*/f32[8,16]{1,0:T(8,128)}) custom-call(bf16[128,1024]{1,0:T(8,128)(2,1)} %q_hbm.1, bf16[128,1024]{1,0:T(8,128)(2,1)} %k_hbm.1, bf16[128,1024]{1,0:T(8,128)(2,1)} %v_hbm.1, s32[1,128]{1,0:T(1,128)} %bitcast.15, ...), custom_call_target="tpu_custom_call" | custom-call | tf_op jit(solution)/shard_map/step/pallas_call | solution.py:958
  68.6 1.6 %spill.1 = (f32[16,1024]{1,0:T(8,128)}, f32[16,1024]{1,0:T(8,128)}, f32[8,16]{1,0:T(8,128)}, f32[16,512]{1,0:T(8,128)}, f32[16,1024]{1,0:T(8,128)}, /*index=5*/f32[8,16]{1,0:T(8,128)}) custom-call(f32[16,1024]{1,0:T(8,128)} %get-tuple-element.18.refs_0_, f32[16,1024]{1,0:T(8,128)} %get-tuple-element.19.refs_1_, f32[8,16]{1,0:T(8,128)} %get-tuple-element.20.refs_2_, ...), custom_call_target="tpu_custom_call" | custom-call | tf_op jit(solution)/shard_map/spill/pallas_call | solution.py:1007

commit v3 on v2

--- a/solution.py
+++ b/solution.py
@@ -304,7 +304,8 @@
 ):
     bf, f32 = jnp.bfloat16, jnp.float32
     count = 2 * chips
-    owners = chips
+    owners = chips // 2
+    share_of = count // owners
     me = lax.axis_index("seq")
     row = lax.axis_index("row")
     other = 1 - row
@@ -366,8 +367,6 @@
     emb[vocab : vocab + rows, :columns] = jnp.zeros((rows, columns), bf)
     emb[:vocab, columns:] = jnp.zeros((vocab, 2 * HEAD), bf)
     emb[vocab + HEAD :] = jnp.zeros((HEAD, wide + HEAD), bf)
-    for buffer in (early, late):
-        buffer[tiles:] = jnp.zeros((count - tiles, rank, HEAD), bf)
 
     pl.semaphore_wait(barrier, len(peers))
 
@@ -556,14 +555,14 @@
     factor = 1.0 / math.sqrt(HEAD) / math.log(2.0)
     span = chips * rows
 
-    def attend(i, late_half):
-        query = qb[i]
+    def attend(pair, late_half):
+        query = jnp.concatenate([qb[i] for i in pair], axis=0)
         start = chips if late_half else 0
         fresh = contract(query, kb[start : start + chips].reshape(span, HEAD), 1, 1)
-        places = lax.broadcasted_iota(jnp.int32, (rows, span), 1)
-        queries = lax.broadcasted_iota(jnp.int32, (rows, span), 0) + (
-            (2 * i + core - start) * rows
-        )
+        places = lax.broadcasted_iota(jnp.int32, (2 * rows, span), 1)
+        queries = lax.broadcasted_iota(jnp.int32, (2 * rows, span), 0)
+        first, second = [(2 * i + core - start) * rows for i in pair]
+        queries = queries + jnp.where(queries < rows, first, second - rows)
         fresh = jnp.where(places <= queries, fresh, -1e30)
         top = jnp.max(fresh, axis=1, keepdims=True)
         if late_half:
@@ -581,36 +580,47 @@
             mixed = mixed + jnp.dot(
                 weights.astype(bf), vb[:start].reshape(span, HEAD), preferred_element_type=f32
             )
-        ob[i] = (mixed / mass).astype(bf)
-
-    @pl.loop(0, chips)
+        mixed = (mixed / mass).astype(bf)
+        for number, i in enumerate(pair):
+            ob[i] = mixed[number * rows : (number + 1) * rows]
+
+    @pl.loop(0, near)
     def _(step):
         @pl.when(step == 1)
         def _():
             relay(2)
             cross_over(1)
 
-        at_home = (step < near - 1) | (step == chips - 1)
-        stage = jnp.where(at_home, lax.rem(step + 1, near), step - (near - 1))
-        i = jnp.where(at_home, home, away) + lax.rem(place_in + near - stage, near)
-
-        @pl.when(i != chip)
+        at_home = step < near // 2
+        stages = (
+            jnp.where(at_home, 2 * step + 1, 2 * step - near),
+            jnp.where(at_home, lax.rem(2 * step + 2, near), 2 * step - near + 1),
+        )
+        pair = [
+            jnp.where(at_home, home, away) + lax.rem(place_in + near - stage, near)
+            for stage in stages
+        ]
+        for i in pair:
+
+            @pl.when(i != chip)
+            def _():
+                landed(2, i)
+
+        @pl.when(pair[0] < near)
         def _():
-            landed(2, i)
-
-        @pl.when(i < near)
+            attend(pair, False)
+
+        @pl.when(pair[0] >= near)
         def _():
-            attend(i, False)
-
-        @pl.when(i >= near)
-        def _():
-            attend(i, True)
-
-        @pl.when(i != chip)
-        def _():
-            remote(
-                ob.at[i], att.at[:, own], o_send.at[i], o_recv.at[chip], 2 * i + core, row
-            ).start()
+            attend(pair, True)
+
+        for i in pair:
+
+            @pl.when(i != chip)
+            def _():
+                remote(
+                    ob.at[i], att.at[:, own], o_send.at[i], o_recv.at[chip], 2 * i + core, row
+                ).start()
 
     att[:, own] = ob[chip]
 
@@ -779,83 +789,106 @@
     )
     small = exact(picks, by_patch, 1, 0)
     small = jnp.concatenate([small, jnp.zeros_like(small)], axis=0)
-    cross[:, :columns] = down.astype(bf)
-    cross[:, columns:] = small.astype(bf)
-    cross_copy = remote(cross, crossr, y_send.at[4], y_recv.at[4], me, other)
-    cross_copy.start()
+    down = down.astype(bf)
     lift = contract(nrm[:, columns:], gr[...], 0, 0)[:rank].astype(bf)
     spread = width // HEAD
     thin = columns // HEAD
     for t in range(spread):
         early[t] = lift[:, t * HEAD : (t + 1) * HEAD]
-    base = owners // 2
-
-    def spread_out(kind, source, landing, first, last):
-        for t in range(first, last):
-            to = base + t
-
-            @pl.when(to != me)
+    for t in range(thin):
+        early[spread + t] = down[:, t * HEAD : (t + 1) * HEAD]
+    early[spread + thin] = small.astype(bf)
+    base = chips // 4
+
+    def owner(t):
+        return 2 * (base + t) + 1
+
+    def held(t):
+        return pl.ds(0, min(share_of, tiles - t * share_of))
+
+    def parcel(kind, t):
+        source, landing = (early, late)[kind], (early_in, late_in)[kind]
+        size = min(share_of, tiles - t * share_of)
+        return remote(
+            source.at[pl.ds(share_of * t, size)], landing.at[me, held(t)], r_send.at[kind, t],
+            r_recv.at[kind, me], owner(t), row,
+        )
+
+    def spread_out(kind):
+        for t in range(owners):
+
+            @pl.when(owner(t) != me)
             def _():
-                remote(
-                    source.at[pl.ds(2 * t, 2)], landing.at[me], r_send.at[kind, t],
-                    r_recv.at[kind, me], to, row,
-                ).start()
-
-            @pl.when(to == me)
+                parcel(kind, t).start()
+
+            @pl.when(owner(t) == me)
             def _():
-                landing[me] = source[2 * t : 2 * t + 2]
-
-    def settle_out(kind, source, landing):
+                size = min(share_of, tiles - t * share_of)
+                source, landing = (early, late)[kind], (early_in, late_in)[kind]
+                landing[me, :size] = source[share_of * t : share_of * t + size]
+
+    def settle_out(kind):
         for t in range(owners):
-            to = base + t
-
-            @pl.when(to != me)
+
+            @pl.when(owner(t) != me)
             def _():
-                remote(
-                    source.at[pl.ds(2 * t, 2)], landing.at[me], r_send.at[kind, t],
-                    r_recv.at[kind, me], to, row,
-                ).wait_send()
-
-    mine = (me >= base) & (me < base + owners)
-    place = jnp.where(mine, me - base, 0)
-
-    def gather_in(kind, landing, final):
-        @pl.when(mine)
-        def _():
-            for d in range(1, count):
-                source = lax.rem(me + d, count)
-                remote(
-                    landing.at[source], landing.at[source], r_send.at[kind, 0],
-                    r_recv.at[kind, source], me, row,
-                ).wait_recv()
-            final[place] = jnp.sum(landing[...].astype(f32), axis=0).astype(bf)
-            for d in range(1, count):
-                to = lax.rem(me + d, count)
-                remote(
-                    final.at[place], final.at[place], g_send.at[kind, d],
-                    g_recv.at[kind, place], to, row,
-                ).start()
+                parcel(kind, t).wait_send()
+
+    def gather_in(kind, final):
+        landing = (early_in, late_in)[kind]
+        for t in range(owners):
+
+            @pl.when(owner(t) == me)
+            def _():
+                size = min(share_of, tiles - t * share_of)
+                for d in range(1, count):
+                    source = lax.rem(me + d, count)
+                    remote(
+                        landing.at[source, held(t)], landing.at[source, held(t)],
+                        r_send.at[kind, 0], r_recv.at[kind, source], me, row,
+                    ).wait_recv()
+                summed = jnp.sum(landing[:, :size].astype(f32), axis=0)
+                if kind == 0 and t * share_of >= spread:
+                    cross[:size] = summed.astype(bf)
+                    swap = remote(
+                        cross.at[held(t)], crossr.at[held(t)], y_send.at[4], y_recv.at[4], me, other
+                    )
+                    swap.start()
+                    swap.wait_recv()
+                    summed = cross[:size].astype(f32) + crossr[:size].astype(f32)
+                final[t, :size] = summed.astype(bf)
+                for d in range(1, count):
+                    issue(kind, final, t, d).start()
+
+    def issue(kind, final, t, d):
+        piece = final.at[t, held(t)]
+        return remote(
+            piece, piece, g_send.at[kind, d], g_recv.at[kind, t], lax.rem(me + d, count), row
+        )
 
     def finish_in(kind, final):
         for t in range(owners):
 
-            @pl.when(me != base + t)
+            @pl.when(owner(t) != me)
             def _():
+                piece = final.at[t, held(t)]
                 remote(
-                    final.at[t], final.at[t], g_send.at[kind, 0], g_recv.at[kind, t], me, row
+                    piece, piece, g_send.at[kind, 0], g_recv.at[kind, t], me, row
                 ).wait_recv()
 
     def settle_in(kind, final):
-        @pl.when(mine)
-        def _():
-            for d in range(1, count):
-                to = lax.rem(me + d, count)
-                remote(
-                    final.at[place], final.at[place], g_send.at[kind, d],
-                    g_recv.at[kind, place], to, row,
-                ).wait_send()
-
-    spread_out(0, early, early_in, 0, spread // 2)
+        for t in range(owners):
+
+            @pl.when(owner(t) == me)
+            def _():
+                for d in range(1, count):
+                    issue(kind, final, t, d).wait_send()
+                if kind == 0 and t * share_of >= spread:
+                    remote(
+                        cross.at[held(t)], crossr.at[held(t)], y_send.at[4], y_recv.at[4], me, other
+                    ).wait_send()
+
+    spread_out(0)
 
     for index in range(pieces):
         patches = pl.ds(index * per_piece, per_piece)
@@ -876,19 +909,13 @@
     for t in range(thin):
         late[spread + t] = pulled[:, t * HEAD : (t + 1) * HEAD]
     late[spread + thin] = tops.astype(bf)
-    spread_out(1, late, late_in, 0, owners)
-    cross_copy.wait_recv()
-    joint = (cross[...].astype(f32) + crossr[...].astype(f32)).astype(bf)
-    for t in range(thin):
-        early[spread + t] = joint[:, t * HEAD : (t + 1) * HEAD]
-    early[spread + thin] = joint[:, columns:]
-    spread_out(0, early, early_in, spread // 2, owners)
-    gather_in(0, early_in, early_full)
-    gather_in(1, late_in, late_full)
+    spread_out(1)
+    gather_in(0, early_full)
+    gather_in(1, late_full)
     finish_in(0, early_full)
 
     def tile_of(final, t):
-        return final[t // 2, t % 2]
+        return final[t // share_of, t % share_of]
 
     for t in range(spread):
         glu_out[:, t * HEAD : (t + 1) * HEAD] = tile_of(early_full, t).astype(f32)
@@ -902,10 +929,8 @@
         bridge[:, t * HEAD : (t + 1) * HEAD] = tile_of(late_full, spread + t)
     ggu_out[...] = contract(bridge[...], lw_ref[...], 1, 1)
     gsc_out[...] = tile_of(late_full, spread + thin)[:TASKS, :rank].astype(f32)
-    for kind, source, landing, final in (
-        (0, early, early_in, early_full), (1, late, late_in, late_full)
-    ):
-        settle_out(kind, source, landing)
+    for kind, final in ((0, early_full), (1, late_full)):
+        settle_out(kind)
         settle_in(kind, final)
     for which, buffer in weights_in:
         for source in range(levels):
@@ -919,7 +944,7 @@
     for source in range(chips):
         for which in range(2):
             share(which, source).wait_send()
-    for copy in [lw_copy, lw_mate, cot_copy, m_copy, red_copy, cross_copy] + e_copies:
+    for copy in [lw_copy, lw_mate, cot_copy, m_copy, red_copy] + e_copies:
         copy.wait_send()
 
 
@@ -985,11 +1010,11 @@
             vm((total, wide), bf), vm((total, HEAD), f32), vm((total, HEAD), f32),
             vm((total, HEAD), f32), vm((total, HEAD), f32), vm((total, width), bf),
             vm((total, HEAD), bf), vm((rows, columns), bf), vm((rows, columns), bf),
-            vm((rank, wide), bf), vm((rank, wide), bf),
+            vm((4, rank, HEAD), bf), vm((4, rank, HEAD), bf),
         ]
         + [
-            vm((count, rank, HEAD), bf), vm((count, 2, rank, HEAD), bf),
-            vm((chips, 2, rank, HEAD), bf),
+            vm((count, rank, HEAD), bf), vm((count, 4, rank, HEAD), bf),
+            vm((chips // 2, 4, rank, HEAD), bf),
         ]
         * 2
         + [

time: 70.4 us -> 68.3 us (0.970)
  Pallas kernels: 69.6 us -> 67.5 us
    pallas_call x1, Pallas kernels: 67.9 us -> 65.9 us  [paired_body(): pl.pallas_call(functools.partial(step_kernel, chips, depth), out_shape=(j...]
where the time goes in v3:
time: 68.3 us; the launch traced here: 68.1 us
  Pallas kernels  67.5 us (99%)
    pallas_call x1, Pallas kernels, paired_body(): pl.pallas_call(functools.partial(step_kernel, chips, depth), out_shape=(j...  65.9 us
    pallas_call x1, Pallas kernels, paired_body(): pl.pallas_call(copy_kernel, out_shape=tuple((jax.ShapeDtypeStruct(item.sh...  1.63 us

profile of v3, /device:TPU:0, one launch (start us, length us, event | category | flops | bytes accessed | tf_op | source)
XLA Modules:
  0.0 68.1 jit_solution(7785511537176203775)
XLA Ops:
  0.6 65.9 %step.1 = (f32[16,1024]{1,0:T(8,128)}, f32[16,1024]{1,0:T(8,128)}, f32[8,16]{1,0:T(8,128)}, f32[16,512]{1,0:T(8,128)}, f32[16,1024]{1,0:T(8,128)}, /*index=5*/f32[8,16]{1,0:T(8,128)}) custom-call(bf16[128,1024]{1,0:T(8,128)(2,1)} %q_hbm.1, bf16[128,1024]{1,0:T(8,128)(2,1)} %k_hbm.1, bf16[128,1024]{1,0:T(8,128)(2,1)} %v_hbm.1, s32[1,128]{1,0:T(1,128)} %bitcast.15, ...), custom_call_target="tpu_custom_call" | custom-call | tf_op jit(solution)/shard_map/step/pallas_call | solution.py:983
  66.5 1.6 %spill.1 = (f32[16,1024]{1,0:T(8,128)}, f32[16,1024]{1,0:T(8,128)}, f32[8,16]{1,0:T(8,128)}, f32[16,512]{1,0:T(8,128)}, f32[16,1024]{1,0:T(8,128)}, /*index=5*/f32[8,16]{1,0:T(8,128)}) custom-call(f32[16,1024]{1,0:T(8,128)} %get-tuple-element.18.refs_0_, f32[16,1024]{1,0:T(8,128)} %get-tuple-element.19.refs_1_, f32[8,16]{1,0:T(8,128)} %get-tuple-element.20.refs_2_, ...), custom_call_target="tpu_custom_call" | custom-call | tf_op jit(solution)/shard_map/spill/pallas_call | solution.py:1032

commit v4 on v3

--- a/solution.py
+++ b/solution.py
@@ -530,6 +530,38 @@
     for to in targets:
         hand(2, to).start()
     cross_over(0)
+    for name in ("res", "gd", "lu", "ld", "table", "tasks", "ids", "pos", "gain", "gs", "ls"):
+        loads[name].wait()
+    picks = (
+        lax.broadcasted_iota(jnp.int32, (TASKS, rows), 0) == tasks_ref[...]
+    ).astype(f32)
+
+    def widen(table):
+        return jnp.concatenate([table, jnp.zeros((TASKS, HEAD - rank), f32)], axis=1)
+
+    task_scales = exact(gs_ref[...], picks, 0, 0)
+    high, low_part = split_pair(exact(picks, widen(ls_ref[...]), 0, 0))
+    emb[vocab : vocab + rows, columns:wide] = high
+    emb[vocab : vocab + rows, wide:] = low_part
+    emb[vocab + rows : vocab + rows + 2 * PATCH, :columns] = jnp.concatenate(
+        [pos_ref[...].astype(f32), jnp.zeros((PATCH, columns), f32)], axis=0
+    ).astype(bf)
+    depth_all = emb.shape[0]
+
+    @pl.loop(0, pieces)
+    def _(index):
+        block = pl.ds(pl.multiple_of(index * SPAN, SPAN), SPAN)
+        line = lax.broadcasted_iota(jnp.int32, (depth_all, SPAN), 0)
+        byte = lax.broadcasted_iota(jnp.int32, (depth_all, SPAN), 1) + index * SPAN
+        chosen = (
+            (line == ids_ref[:, block])
+            | (line == vocab + byte // PATCH)
+            | (line == vocab + rows + lax.rem(byte, PATCH))
+        )
+        found = contract(jnp.where(chosen, 1.0, 0.0).astype(bf), emb[...], 0, 0)
+        inp[block] = found[:, :columns]
+        sca[block] = found[:, columns:wide] + found[:, wide:]
+
     for j in range(1, near):
         source = home + lax.rem(place_in + near - j, near)
         for which in range(2):
@@ -635,24 +667,8 @@
         )
         w2[block] = summed.astype(bf)
 
-    for name in ("res", "gd", "lu", "ld", "table", "tasks", "ids", "pos", "gain", "gs", "ls"):
-        loads[name].wait()
-    picks = (
-        lax.broadcasted_iota(jnp.int32, (TASKS, rows), 0) == tasks_ref[...]
-    ).astype(f32)
-
-    def widen(table):
-        return jnp.concatenate([table, jnp.zeros((TASKS, HEAD - rank), f32)], axis=1)
-
-    task_scales = exact(gs_ref[...], picks, 0, 0)
-    high, low_part = split_pair(exact(picks, widen(ls_ref[...]), 0, 0))
-    emb[vocab : vocab + rows, columns:wide] = high
-    emb[vocab : vocab + rows, wide:] = low_part
-    emb[vocab + rows : vocab + rows + 2 * PATCH, :columns] = jnp.concatenate(
-        [pos_ref[...].astype(f32), jnp.zeros((PATCH, columns), f32)], axis=0
-    ).astype(bf)
     direct = jnp.dot(res_ref[...], lw_ref[...], preferred_element_type=f32)
-    inp[:rows] = direct
+    lif[...] = direct
 
     cot_copy.wait_recv()
     m_copy.wait_recv()
@@ -670,6 +686,14 @@
         for index in range(2)
     )
 
+    def mates_weights_of(which, source):
+        for line in (side, 1 - side):
+            to_mate(which, source, line).wait_recv()
+
+    def turn(source):
+        lanes = pl.ds(pl.multiple_of(source * 2 * depth * shard, HEAD), 2 * depth * shard)
+        wit[:, lanes] = jnp.transpose(wi[lanes])
+
     for hop in range(3, levels):
         relay(hop)
     for hop in range(2, levels - 1):
@@ -689,19 +713,30 @@
     red_copy = remote(red, redr, y_send.at[3], y_recv.at[3], me, other)
     red_copy.start()
     e1[...] = (
-        jnp.dot(att[...], w2[...], preferred_element_type=f32) + inp[:rows]
+        jnp.dot(att[...], w2[...], preferred_element_type=f32) + lif[...]
     ).astype(bf)
     for index in range(pieces):
         patches = pl.ds(index * per_piece, per_piece)
         copy = remote(e1.at[patches], e1r.at[patches], e_send.at[index], e_recv.at[index], me, other)
         copy.start()
         e_copies.append(copy)
+    mates_weights_of(0, level)
+    for hop in range(1, levels - 1):
+        for source in (level - hop, level + hop):
+
+            @pl.when((source >= 0) & (source < levels))
+            def _():
+                mates_weights_of(0, source)
+                turn(source)
+
+    cross_over(levels - 1)
+    turn(level)
+    wit[:, columns:] = jnp.transpose(wi[columns:])
     red_copy.wait_recv()
     reduced = red[...].astype(f32) + redr[...].astype(f32)
     scaled = (reduced * task_scales).astype(bf)
     lifted = contract(scaled, bridge[...], 0, 0)
 
-    depth_all = emb.shape[0]
     lif[...] = lifted
 
     @pl.loop(0, pieces)
@@ -711,42 +746,33 @@
         remote(
             e1.at[patches], e1r.at[patches], e_send.at[index], e_recv.at[index], me, other
         ).wait_recv()
-        emb[pl.ds(pl.multiple_of(vocab + index * per_piece, per_piece), per_piece), :columns] = (
+        projected = (
             e1[patches].astype(f32) + e1r[patches].astype(f32) + lif[patches]
         ).astype(bf)
-
-        @pl.when(index == pieces // 2)
-        def _():
-            cross_over(levels - 1)
-
-        line = lax.broadcasted_iota(jnp.int32, (depth_all, SPAN), 0)
-        byte = lax.broadcasted_iota(jnp.int32, (depth_all, SPAN), 1) + index * SPAN
-        chosen = (
-            (line == ids_ref[:, block])
-            | (line == vocab + byte // PATCH)
-            | (line == vocab + rows + lax.rem(byte, PATCH))
-        )
-        found = contract(jnp.where(chosen, 1.0, 0.0).astype(bf), emb[...], 0, 0)
-        inputs = found[:, :columns]
-        scales = found[:, columns:wide] + found[:, wide:]
+        near_by = (
+            lax.broadcasted_iota(jnp.int32, (per_piece, SPAN), 1) // PATCH
+            == lax.broadcasted_iota(jnp.int32, (per_piece, SPAN), 0)
+        ).astype(f32).astype(bf)
+        inputs = inp[block] + contract(near_by, projected, 0, 0)
+        scales = sca[block]
         inverse = lax.rsqrt(jnp.mean(inputs * inputs, axis=1, keepdims=True) + 1e-06)
         normed = (inputs * inverse * gain_ref[...]).astype(bf)
         lowered = contract(normed, ld_ref[...], 1, 1)
         inp[block] = inputs
         inv[block] = jnp.broadcast_to(inverse, (SPAN, HEAD))
-        sca[block] = scales
         low[block] = lowered
         nrm[block, :columns] = normed
         nrm[block, columns:] = (lowered * scales).astype(bf)
 
-    def mates_weights(which):
-        for source in range(levels):
-            for line in (side, 1 - side):
-                to_mate(which, source, line).wait_recv()
-
-    mates_weights(1)
-    mates_weights(0)
-    wit[...] = jnp.transpose(wi[...])
+    for source in range(levels):
+        mates_weights_of(1, source)
+    for source in (level - (levels - 1), level + (levels - 1)):
+
+        @pl.when((source >= 0) & (source < levels))
+        def _():
+            mates_weights_of(0, source)
+            turn(source)
+
     @pl.loop(0, pieces)
     def _(index):
         block = pl.ds(pl.multiple_of(index * SPAN, SPAN), SPAN)
@@ -922,16 +948,9 @@
     for t in range(thin):
         gld_out[:, t * HEAD : (t + 1) * HEAD] = tile_of(early_full, spread + t).astype(f32)
     lsc_out[...] = tile_of(early_full, spread + thin)[:TASKS, :rank].astype(f32)
-    finish_in(1, late_full)
-    for t in range(spread):
-        ggd_out[:, t * HEAD : (t + 1) * HEAD] = tile_of(late_full, t).astype(f32)
-    for t in range(thin):
-        bridge[:, t * HEAD : (t + 1) * HEAD] = tile_of(late_full, spread + t)
-    ggu_out[...] = contract(bridge[...], lw_ref[...], 1, 1)
-    gsc_out[...] = tile_of(late_full, spread + thin)[:TASKS, :rank].astype(f32)
-    for kind, final in ((0, early_full), (1, late_full)):
-        settle_out(kind)
-        settle_in(kind, final)
+    settle_out(0)
+    settle_in(0, early_full)
+    settle_out(1)
     for which, buffer in weights_in:
         for source in range(levels):
             settle_along(which, source)
@@ -946,6 +965,14 @@
             share(which, source).wait_send()
     for copy in [lw_copy, lw_mate, cot_copy, m_copy, red_copy] + e_copies:
         copy.wait_send()
+    finish_in(1, late_full)
+    for t in range(spread):
+        ggd_out[:, t * HEAD : (t + 1) * HEAD] = tile_of(late_full, t).astype(f32)
+    for t in range(thin):
+        bridge[:, t * HEAD : (t + 1) * HEAD] = tile_of(late_full, spread + t)
+    ggu_out[...] = contract(bridge[...], lw_ref[...], 1, 1)
+    gsc_out[...] = tile_of(late_full, spread + thin)[:TASKS, :rank].astype(f32)
+    settle_in(1, late_full)
 
 
 def copy_kernel(*refs):

time: 68.3 us -> 67.1 us (0.982)
  Pallas kernels: 67.5 us -> 66.3 us
    pallas_call x1, Pallas kernels: 65.9 us -> 64.6 us  [paired_body(): pl.pallas_call(functools.partial(step_kernel, chips, depth), out_shape=(j...]
where the time goes in v4:
time: 67.1 us; the launch traced here: 66.9 us
  Pallas kernels  66.3 us (99%)
    pallas_call x1, Pallas kernels, paired_body(): pl.pallas_call(functools.partial(step_kernel, chips, depth), out_shape=(j...  64.6 us
    pallas_call x1, Pallas kernels, paired_body(): pl.pallas_call(copy_kernel, out_shape=tuple((jax.ShapeDtypeStruct(item.sh...  1.63 us

profile of v4, /device:TPU:0, one launch (start us, length us, event | category | flops | bytes accessed | tf_op | source)
XLA Modules:
  0.0 66.9 jit_solution(11775243623879045348)
XLA Ops:
  0.6 64.6 %step.1 = (f32[16,1024]{1,0:T(8,128)}, f32[16,1024]{1,0:T(8,128)}, f32[8,16]{1,0:T(8,128)}, f32[16,512]{1,0:T(8,128)}, f32[16,1024]{1,0:T(8,128)}, /*index=5*/f32[8,16]{1,0:T(8,128)}) custom-call(bf16[128,1024]{1,0:T(8,128)(2,1)} %q_hbm.1, bf16[128,1024]{1,0:T(8,128)(2,1)} %k_hbm.1, bf16[128,1024]{1,0:T(8,128)(2,1)} %v_hbm.1, s32[1,128]{1,0:T(1,128)} %bitcast.15, ...), custom_call_target="tpu_custom_call" | custom-call | tf_op jit(solution)/shard_map/step/pallas_call | solution.py:1010
  65.3 1.6 %spill.1 = (f32[16,1024]{1,0:T(8,128)}, f32[16,1024]{1,0:T(8,128)}, f32[8,16]{1,0:T(8,128)}, f32[16,512]{1,0:T(8,128)}, f32[16,1024]{1,0:T(8,128)}, /*index=5*/f32[8,16]{1,0:T(8,128)}) custom-call(f32[16,1024]{1,0:T(8,128)} %get-tuple-element.18.refs_0_, f32[16,1024]{1,0:T(8,128)} %get-tuple-element.19.refs_1_, f32[8,16]{1,0:T(8,128)} %get-tuple-element.20.refs_2_, ...), custom_call_target="tpu_custom_call" | custom-call | tf_op jit(solution)/shard_map/spill/pallas_call | solution.py:1059

commit v5 on v4

--- a/solution.py
+++ b/solution.py
@@ -618,7 +618,7 @@
 
     @pl.loop(0, near)
     def _(step):
-        @pl.when(step == 1)
+        @pl.when(step == near // 2)
         def _():
             relay(2)
             cross_over(1)

time: 67.1 us -> 66.8 us (level)
  no operation moved by 1% of the time
where the time goes in v5:
time: 66.8 us; the launch traced here: 66.7 us
  Pallas kernels  66 us (99%)
    pallas_call x1, Pallas kernels, paired_body(): pl.pallas_call(functools.partial(step_kernel, chips, depth), out_shape=(j...  64.4 us
    pallas_call x1, Pallas kernels, paired_body(): pl.pallas_call(copy_kernel, out_shape=tuple((jax.ShapeDtypeStruct(item.sh...  1.63 us

profile of v5, /device:TPU:0, one launch (start us, length us, event | category | flops | bytes accessed | tf_op | source)
XLA Modules:
  0.0 66.7 jit_solution(12879765717952225385)
XLA Ops:
  0.6 64.4 %step.1 = (f32[16,1024]{1,0:T(8,128)}, f32[16,1024]{1,0:T(8,128)}, f32[8,16]{1,0:T(8,128)}, f32[16,512]{1,0:T(8,128)}, f32[16,1024]{1,0:T(8,128)}, /*index=5*/f32[8,16]{1,0:T(8,128)}) custom-call(bf16[128,1024]{1,0:T(8,128)(2,1)} %q_hbm.1, bf16[128,1024]{1,0:T(8,128)(2,1)} %k_hbm.1, bf16[128,1024]{1,0:T(8,128)(2,1)} %v_hbm.1, s32[1,128]{1,0:T(1,128)} %bitcast.15, ...), custom_call_target="tpu_custom_call" | custom-call | tf_op jit(solution)/shard_map/step/pallas_call | solution.py:1010
  65.0 1.6 %spill.1 = (f32[16,1024]{1,0:T(8,128)}, f32[16,1024]{1,0:T(8,128)}, f32[8,16]{1,0:T(8,128)}, f32[16,512]{1,0:T(8,128)}, f32[16,1024]{1,0:T(8,128)}, /*index=5*/f32[8,16]{1,0:T(8,128)}) custom-call(f32[16,1024]{1,0:T(8,128)} %get-tuple-element.18.refs_0_, f32[16,1024]{1,0:T(8,128)} %get-tuple-element.19.refs_1_, f32[8,16]{1,0:T(8,128)} %get-tuple-element.20.refs_2_, ...), custom_call_target="tpu_custom_call" | custom-call | tf_op jit(solution)/shard_map/spill/pallas_call | solution.py:1059
